TPU v7x, 256 devices: a whole 4x4x8 slice. The times are simulated.
256 devices in a mesh: row: 8 (over x, y_hi), col: 32 (over z, y_lo, core).
Axes of the slice: x: 4, y: 4 (y_hi: 2, y_lo: 2; y = y_hi * 2 + y_lo), z: 8, core: 2. Of those that a mesh axis runs over, the one named last changes fastest.
Arguments:
- boxes: int32 [4, 65536], P(None, 'col'), may hold values from 0 to 4095, as said below
- pins: int32 [65536], P('col'), may hold values from 2 to 64
- capacity: float32 [4096, 4096], P('row', 'col'), may hold values from 4 to 12
- cell_bin: int32 [8, 65536], P('row', 'col'), may hold values from 0 to 65535
- cell_area: float32 [8, 65536], P('row', 'col'), may hold values from 1 to 10
Outputs:
- rudy: float32 [4096, 4096], P('row', 'col')
- inflation: float32 [4096, 4096], P('row', 'col')
- cell_sizes: float32 [8, 65536], P('row', 'col')
Inputs may be any that keep to these rules, and one draw needn't show every extreme that they name: `boxes`: row 0 and 1 are a net's first and last bin column, row 2 and 3 its first and last bin row; first <= last, a box spans at most 512 columns and 512 rows.
All inputs are finite; a program needn't handle non-finite values.
Results may differ from a plain program's by a relative error of at most 0.0003.
Values sent between devices are 32-bit elements; how exact they have to be, the bound alone decides.
No kernel may reach another device: no remote copies, remote signals or barrier semaphores. Data moves between devices by JAX's collectives and lax.ppermute only.
A program may use at most 64 MiB of HBM per device.

v0:
```python
import functools

import jax
import jax.numpy as jnp
from jax import lax
from jax.sharding import Mesh
from jax.sharding import PartitionSpec as P

ROW = ("row_0", "row_1")
COL = ("col_0", "col_1", "col_2")
ROW_COL = ("row_0", "row_1", "col_0", "col_1", "col_2")


def joined_along(pieces, dim):
    pieces = jnp.moveaxis(pieces, 0, dim)
    dims = pieces.shape
    return pieces.reshape(*dims[:dim], dims[dim] * dims[dim + 1], *dims[dim + 2 :])


def copy_for_each(shard, axis):
    peers = lax.axis_size(axis)
    return lax.all_to_all(
        jnp.broadcast_to(shard[None], (peers, *shard.shape)), axis, 0, 0, tiled=True
    )


def collect(shard, axis, dim):
    return joined_along(copy_for_each(shard, axis), dim)


def one_axis_at_a_time(shard, axes):
    return functools.reduce(lax.psum, axes, shard)


def raster(table, row_start, row_count, col_count):
    total_nets = table.shape[1]
    block = 512
    rows_here = row_start + jnp.arange(row_count, dtype=jnp.int32)
    cols_here = jnp.arange(col_count, dtype=jnp.int32)

    def add_block(index, acc):
        piece = lax.dynamic_slice_in_dim(table, index * block, block, 1)
        first_x, last_x, first_y, last_y, count = (piece[0], piece[1], piece[2], piece[3], piece[4])
        span_x = (last_x - first_x + 1).astype(jnp.float32)
        span_y = (last_y - first_y + 1).astype(jnp.float32)
        weight = (
            jnp.log(count.astype(jnp.float32)) * (span_x + span_y) / (span_x * span_y)
        ).astype(jnp.bfloat16)
        row_hits = (
            (rows_here[None, :] >= first_y[:, None]) & (rows_here[None, :] <= last_y[:, None])
        ).astype(jnp.bfloat16)
        col_hits = (cols_here[None, :] >= first_x[:, None]) & (
            cols_here[None, :] <= last_x[:, None]
        )
        weighted = jnp.where(col_hits, weight[:, None], jnp.zeros((), jnp.bfloat16))
        return acc + lax.dot_general(
            row_hits, weighted, (((0,), (0,)), ((), ())), preferred_element_type=jnp.float32
        )

    empty = jnp.zeros((row_count, col_count), jnp.float32)
    return lax.fori_loop(0, total_nets // block, add_block, empty)


def per_device(boxes, pins, capacity, cell_bin, cell_area):
    tile_rows, tile_cols = capacity.shape
    row_start = lax.axis_index(ROW) * tile_rows
    table = jnp.concatenate([boxes, pins[None, :]], axis=0)
    band = raster(table, row_start, tile_rows, tile_cols * lax.axis_size(COL))
    rudy = lax.psum_scatter(band, COL, scatter_dimension=1, tiled=True)
    excess = jnp.maximum(rudy - capacity, 0.0)
    ladder = jnp.arange(tile_rows, dtype=jnp.int32)
    lower = (ladder[:, None] >= ladder[None, :]).astype(jnp.float32)
    within = jnp.dot(
        lower, excess, precision=lax.Precision.HIGHEST, preferred_element_type=jnp.float32
    )
    column_sum = within[-1]
    stacked = collect(column_sum[None, :], ROW, 0)
    above = jnp.arange(stacked.shape[0], dtype=jnp.int32) < lax.axis_index(ROW)
    carried = jnp.sum(jnp.where(above[:, None], stacked, 0.0), axis=0)
    prefix = within + carried[None, :]
    grid_rows = tile_rows * lax.axis_size(ROW)
    inflation = 1.0 + 2.0 * prefix / grid_rows
    looked = jnp.take(inflation.reshape(-1), cell_bin[0], axis=0)
    grown = cell_area * looked[None, :]
    area_sum, grown_sum = (
        one_axis_at_a_time(jnp.sum(cell_area), ROW_COL),
        one_axis_at_a_time(jnp.sum(grown), ROW_COL),
    )
    cell_sizes = grown * (area_sum / grown_sum)
    return (rudy, inflation, cell_sizes)


def solution(mesh):
    split = Mesh(mesh.devices.reshape(4, 2, 8, 2, 2), ("row_0", "row_1", "col_0", "col_1", "col_2"))
    placed = (P(None, COL), P(COL), P(ROW, COL), P(ROW, COL), P(ROW, COL))
    return jax.shard_map(
        per_device,
        mesh=split,
        in_specs=placed,
        out_specs=(P(ROW, COL), P(ROW, COL), P(ROW, COL)),
        check_vma=False,
    )
```

profile of v0, /device:TPU:1, one launch (start us, length us, event | category | flops | bytes accessed | tf_op | source)
XLA Modules:
  0.0 262.5 jit_solution(17198931388420724391)
XLA Ops:
  7.2 0.0 reduce-scatter.2.cloned.1.call-start
  7.2 0.8 pad_add_fusion
  8.0 40.2 %while.15 = (s32[]{:T(128)}, f32[512,4096]{1,0:T(8,128)}, s32[5,2048]{1,0:T(8,128)S(1)}, s32[]{:T(128)}, s32[]{:T(128)}, /*index=5*/s32[]{:T(128)}, s32[]{}, s32[]{:T(128)}, s32[]{:T(128)}, s32[]{}, /*index=10*/s32[]{}, s32[]{}) while((s32[]{:T(128)}, f32[512,4096]{1,0:T(8,128)}, s32[5,2048]{1,0:T(8,128)S(1)}, ...), condition=%wide.region_1.2_spmd.clone.clone, body=%wide.region_0.1_spmd.clone.clone.sunk | while | flops 2160859648 | bytes 16822520 | solution.py:61
  8.0 0.1 fusion.37
  8.1 0.1 fusion.38
  8.3 7.3 %select_add_fusion.2 = f32[512,4096]{1,0:T(8,128)} fusion(f32[512,4096]{1,0:T(8,128)} %get-tuple-element.206, s32[512]{0:T(512)S(1)} %bitcast.28, s32[512]{0:T(512)S(1)} %bitcast.30, pred[]{:T(512)S(6)} %compare.3, bf16[512]{0:T(512)(128)(2,1)S(1)} %fusion.39, s32[512]{0:T(512)S(1)} %iota_add_fusion.2, s32[512]{0:T(512)S(1)} %bitcast.32, ...), kind=kOutput, calls=%fused_computation.5.clone.1 | convolution fusion | flops 2160852992 | bytes 16788480 | tf_op jit(solution)/shard_map/while/body/eval_jaxpr/dot_general | solution.py:56
  15.6 0.1 fusion.37
  15.6 0.1 fusion.38
  15.8 10.7 %select_add_fusion.2 = f32[512,4096]{1,0:T(8,128)} fusion(f32[512,4096]{1,0:T(8,128)} %get-tuple-element.206, s32[512]{0:T(512)S(1)} %bitcast.28, s32[512]{0:T(512)S(1)} %bitcast.30, pred[]{:T(512)S(6)} %compare.3, bf16[512]{0:T(512)(128)(2,1)S(1)} %fusion.39, s32[512]{0:T(512)S(1)} %iota_add_fusion.2, s32[512]{0:T(512)S(1)} %bitcast.32, ...), kind=kOutput, calls=%fused_computation.5.clone.1 | convolution fusion | flops 2160852992 | bytes 16788480 | tf_op jit(solution)/shard_map/while/body/eval_jaxpr/dot_general | solution.py:56
  26.5 0.1 fusion.37
  26.5 0.1 fusion.38
  26.7 10.7 %select_add_fusion.2 = f32[512,4096]{1,0:T(8,128)} fusion(f32[512,4096]{1,0:T(8,128)} %get-tuple-element.206, s32[512]{0:T(512)S(1)} %bitcast.28, s32[512]{0:T(512)S(1)} %bitcast.30, pred[]{:T(512)S(6)} %compare.3, bf16[512]{0:T(512)(128)(2,1)S(1)} %fusion.39, s32[512]{0:T(512)S(1)} %iota_add_fusion.2, s32[512]{0:T(512)S(1)} %bitcast.32, ...), kind=kOutput, calls=%fused_computation.5.clone.1 | convolution fusion | flops 2160852992 | bytes 16788480 | tf_op jit(solution)/shard_map/while/body/eval_jaxpr/dot_general | solution.py:56
  37.3 0.1 fusion.37
  37.4 0.1 fusion.38
  37.5 10.7 %select_add_fusion.2 = f32[512,4096]{1,0:T(8,128)} fusion(f32[512,4096]{1,0:T(8,128)} %get-tuple-element.206, s32[512]{0:T(512)S(1)} %bitcast.28, s32[512]{0:T(512)S(1)} %bitcast.30, pred[]{:T(512)S(6)} %compare.3, bf16[512]{0:T(512)(128)(2,1)S(1)} %fusion.39, s32[512]{0:T(512)S(1)} %iota_add_fusion.2, s32[512]{0:T(512)S(1)} %bitcast.32, ...), kind=kOutput, calls=%fused_computation.5.clone.1 | convolution fusion | flops 2160852992 | bytes 16788480 | tf_op jit(solution)/shard_map/while/body/eval_jaxpr/dot_general | solution.py:56
  48.2 0.0 copy-start.1
  48.2 0.0 copy-start
  48.2 0.0 copy-start.2
  48.2 0.0 reduce-scatter.2.cloned.1.call-update
  48.3 0.7 copy-done.1
  49.0 131.8 %reduce-scatter.2.cloned.1.call-done = f32[512,128]{1,0:T(8,128)} async-done(((f32[512,4096]{1,0:T(8,128)}), f32[512,128]{1,0:T(8,128)}) %reduce-scatter.2.cloned.1.call-update) | async-done | bytes 262160 | tf_op jit(solution)/shard_map/reduce_scatter | solution.py:69
  180.7 0.0 copy-done
  180.7 1.6 fusion.20
  182.3 0.6 broadcast_in_dim.77
  182.9 6.0 %all-to-all-start = ((f32[8,1,128]{2,1,0:T(1,128)}), f32[8,1,128]{2,1,0:T(1,128)S(1)}, u32[]{:S(2)}, u32[]{:S(2)}) async-start(f32[8,1,128]{2,1,0:T(1,128)} %broadcast_in_dim.77), calls=%async_computation.1 | async-start | bytes 8192 | tf_op jit(solution)/shard_map/all_to_all | solution.py:22
  189.0 6.4 %all-to-all-done = f32[8,1,128]{2,1,0:T(1,128)S(1)} async-done(((f32[8,1,128]{2,1,0:T(1,128)}), f32[8,1,128]{2,1,0:T(1,128)S(1)}, u32[]{:S(2)}, u32[]{:S(2)}) %all-to-all-start) | async-done | bytes 4128 | tf_op jit(solution)/shard_map/all_to_all | solution.py:22
  195.4 0.1 select_reduce_fusion
  195.5 0.7 multiply_add_fusion
  196.3 11.8 %gather_fusion = f32[2048]{0:T(1024)S(1)} fusion(f32[65536]{0:T(1024)S(1)} %fusion.29, s32[2048]{0:T(1024)S(1)} %broadcast_clamp_fusion), kind=kCustom, calls=%fused_computation | custom fusion | bytes 24576 | tf_op jit(solution)/shard_map/jit(_take)/gather | solution.py:83
  208.0 0.0 copy-done.2
  208.1 0.6 fusion.26
  208.7 7.6 %all-reduce.1 = (f32[]{:T(128)}, f32[]{:T(128)}) all-reduce(f32[]{:T(128)} %get-tuple-element.159, f32[]{:T(128)} %get-tuple-element.153), channel_id=1, replica_groups=mesh['row_0'=4,'row_1'=2,'col_0'=8,'col_1'=2,'col_2'=2] {'row_0'}, use_global_device_ids=true, to_apply=%region_5.6 | all-reduce | flops 2 | bytes 16 | tf_op jit(solution)/shard_map/psum | solution.py:32
  216.3 5.9 %all-reduce.4 = (f32[]{:T(128)}, f32[]{:T(128)}) all-reduce(f32[]{:T(128)} %get-tuple-element.145, f32[]{:T(128)} %get-tuple-element.146), channel_id=1, replica_groups=mesh['row_0'=4,'row_1'=2,'col_0'=8,'col_1'=2,'col_2'=2] {'row_1'}, use_global_device_ids=true, to_apply=%region_6.7 | all-reduce | flops 2 | bytes 16 | tf_op jit(solution)/shard_map/psum | solution.py:32
  222.1 12.6 %all-reduce = (f32[]{:T(128)}, f32[]{:T(128)}) all-reduce(f32[]{:T(128)} %get-tuple-element.151, f32[]{:T(128)} %get-tuple-element.152), channel_id=1, replica_groups=mesh['row_0'=4,'row_1'=2,'col_0'=8,'col_1'=2,'col_2'=2] {'col_0'}, use_global_device_ids=true, to_apply=%region_7.8 | all-reduce | flops 2 | bytes 16 | tf_op jit(solution)/shard_map/psum | solution.py:32
  234.8 6.5 %all-reduce.3 = (f32[]{:T(128)}, f32[]{:T(128)}) all-reduce(f32[]{:T(128)} %get-tuple-element.143, f32[]{:T(128)} %get-tuple-element.144), channel_id=1, replica_groups=mesh['row_0'=4,'row_1'=2,'col_0'=8,'col_1'=2,'col_2'=2] {'col_1'}, use_global_device_ids=true, to_apply=%region_8.9 | all-reduce | flops 2 | bytes 16 | tf_op jit(solution)/shard_map/psum | solution.py:32
  241.3 12.4 %all-reduce.2 = (f32[]{:T(128)}, f32[]{:T(128)}) all-reduce(f32[]{:T(128)} %get-tuple-element.149, f32[]{:T(128)} %get-tuple-element.150), channel_id=1, replica_groups=mesh['row_0'=4,'row_1'=2,'col_0'=8,'col_1'=2,'col_2'=2] {'col_2'}, use_global_device_ids=true, to_apply=%region_9.10 | all-reduce | flops 2 | bytes 16 | tf_op jit(solution)/shard_map/psum | solution.py:32
  255.1 0.6 broadcast_multiply_fusion
  (14 shorter events, 0.1 us)
Async XLA Ops:
  7.2 173.6 %reduce-scatter.2.cloned.1.call-start = ((), (), s32[]{:S(2)}) async-start(), calls=%async_computation.2 | async-start | bytes 8650752 | tf_op jit(solution)/shard_map/reduce_scatter | solution.py:69
  48.2 0.7 copy-start.1
  48.2 132.5 %copy-start = (f32[512,128]{1,0:T(8,128)S(1)}, f32[512,128]{1,0:T(8,128)}, u32[]{:S(2)}) copy-start(f32[512,128]{1,0:T(8,128)} %param.9) | copy-start | bytes 786436
  48.2 159.8 %copy-start.2 = (f32[1,2048]{1,0:T(1,128)S(1)}, f32[1,2048]{1,0:T(1,128)}, u32[]{:S(2)}) copy-start(f32[1,2048]{1,0:T(1,128)} %param.11) | copy-start | bytes 24580
  182.9 12.5 %all-to-all-start = ((f32[8,1,128]{2,1,0:T(1,128)}), f32[8,1,128]{2,1,0:T(1,128)S(1)}, u32[]{:S(2)}, u32[]{:S(2)}) async-start(f32[8,1,128]{2,1,0:T(1,128)} %broadcast_in_dim.77), calls=%async_computation.1 | async-start | bytes 8192 | tf_op jit(solution)/shard_map/all_to_all | solution.py:22
Sparse Core Ops, SparseCore 0:
  48.4 132.3 reduce-scatter.1
where the time goes:
time: 263 us
  waiting for transfers between devices  138 us (52%)
  blocking collectives  45 us (17%)
  matrix products  40.9 us (16%)
  between operations  15.5 us (6%)
  local copies, waits for them, and re-layouts  13.4 us (5%)
  starting transfers between devices  6.08 us (2%)
  other arithmetic  3.3 us (1%)
    reduce_scatter x1, waiting for transfers between devices, per_device(): rudy = lax.psum_scatter(band, COL, scatter_dimension=1, tiled=True)  132 us
    psum x5, blocking collectives, one_axis_at_a_time(): return functools.reduce(lax.psum, axes, shard)  45 us
    dot_general x4, matrix products, add_block(): lax.dot_general(row_hits, weighted, (((0,), (0,)), ((), ())), preferred_e...  39.4 us
    gather x1, local copies, waits for them, and re-layouts, per_device(): looked = jnp.take(inflation.reshape(-1), cell_bin[0], axis=0)  11.8 us
    all_to_all x1, waiting for transfers between devices, copy_for_each(): lax.all_to_all(jnp.broadcast_to(shard[None], (peers, *shard.shape)), axis...  6.45 us
    all_to_all x1, starting transfers between devices, copy_for_each(): lax.all_to_all(jnp.broadcast_to(shard[None], (peers, *shard.shape)), axis...  6.04 us
  transfers between devices with their start and end apart: 2, of which 2 were waited for; matrix products, arithmetic and copies ran while one was open for 0% of the time, Pallas kernels for 0%

commit v1 on v0

v1 whole, which is shorter than its diff:
```python
import functools

import jax
import jax.numpy as jnp
from jax import lax
from jax.experimental import pallas as pl
from jax.experimental.pallas import tpu as pltpu
from jax.sharding import Mesh
from jax.sharding import PartitionSpec as P

ROW = ("row_0", "row_1")
COL = ("col_0", "col_1", "col_2")
SLOTS = 128
LANES = 128
F32 = jnp.float32
BF16 = jnp.bfloat16


def iota(shape, dim):
    return lax.broadcasted_iota(jnp.int32, shape, dim)


def contract(a, b, dim_a, dim_b):
    return lax.dot_general(
        a, b, (((dim_a,), (dim_b,)), ((), ())), preferred_element_type=F32
    )


def three_parts(x):
    high = x.astype(BF16)
    rest = x - high.astype(F32)
    middle = rest.astype(BF16)
    low = (rest - middle.astype(F32)).astype(BF16)
    return high, middle, low


def pack_kernel(peers, groups, group_cols, tile_rows, info_ref, boxes_ref, pins_ref, out_ref, vals_ref):
    nets = boxes_ref.shape[1]
    row_start = info_ref[0]
    base = info_ref[1]
    first_x, last_x = boxes_ref[0:1, :], boxes_ref[1:2, :]
    first_y, last_y = boxes_ref[2:3, :], boxes_ref[3:4, :]
    span_x = (last_x - first_x + 1).astype(F32)
    span_y = (last_y - first_y + 1).astype(F32)
    weight = jnp.log(pins_ref[...].astype(F32)) * (span_x + span_y) / (span_x * span_y)
    weight = weight.astype(BF16).astype(F32)
    vals_ref[...] = jnp.zeros_like(vals_ref)
    vals_ref[0:4, :] = lax.shift_right_logical(boxes_ref[...], 8).astype(F32)
    vals_ref[4:5, :] = weight * (1.0 / 256.0)
    vals_ref[8:12, :] = (boxes_ref[...] & 255).astype(F32)
    vals = vals_ref[...].astype(BF16)

    group_at = iota((groups, nets), 0) * group_cols
    in_band = (first_y < row_start + tile_rows) & (last_y >= row_start)
    hit = (
        jnp.broadcast_to(in_band, (groups, nets))
        & (first_x < group_at + group_cols)
        & (last_x >= group_at)
    )
    hit = jnp.where(hit, 1.0, 0.0)
    chunks = nets // LANES
    stacked = jnp.concatenate(
        [hit[:, k * LANES : (k + 1) * LANES] for k in range(chunks)], axis=0
    ).astype(BF16)
    below = (iota((LANES, LANES), 0) < iota((LANES, LANES), 1)).astype(F32).astype(BF16)
    before = contract(stacked, below, 1, 0)
    whole = contract(stacked, jnp.ones((LANES, LANES), BF16), 1, 0)
    offset = jnp.zeros((groups, LANES), F32)
    ranks = []
    for k in range(chunks):
        rows = slice(k * groups, (k + 1) * groups)
        ranks.append(before[rows] + offset)
        offset = offset + whole[rows]
    rank = jnp.concatenate(ranks, axis=1)
    rank = jnp.where(hit > 0.0, rank - base.astype(F32), -1.0)
    largest = jnp.max(offset, axis=0, keepdims=True)

    slot = iota((SLOTS, nets), 0).astype(F32)
    field = iota((8, SLOTS), 0)
    for group in range(groups):
        chosen = jnp.where(slot == rank[group : group + 1, :], 1.0, 0.0).astype(BF16)
        got = contract(vals, chosen, 1, 1)
        row = got[0:8] * 256.0 + got[8:16]
        row = jnp.where(field == 5, jnp.broadcast_to(largest, (8, SLOTS)), row)
        for peer in range(group * (peers // groups), (group + 1) * (peers // groups)):
            out_ref[peer] = row


def tile_kernel(
    row_peers,
    info_ref,
    nets_ref,
    past_ref,
    capacity_ref,
    bins_ref,
    area_ref,
    rudy_ref,
    within_ref,
    looked_ref,
    pay_ref,
    hits_ref,
    cols_ref,
):
    tile_rows, tile_cols = capacity_ref.shape
    row_start = info_ref[0]
    col_start = info_ref[1]
    first_round = info_ref[2]
    peers = nets_ref.shape[0]
    row_at = (iota((tile_rows, SLOTS), 0) + row_start).astype(F32)
    col_at = (iota((tile_cols, SLOTS), 0) + col_start).astype(F32)
    largest = jnp.zeros((1, SLOTS), F32)
    for peer in range(peers):
        box = nets_ref[peer]
        first_x, last_x = box[0:1], box[1:2]
        first_y, last_y = box[2:3], box[3:4]
        weight = box[4:5]
        largest = jnp.maximum(largest, box[5:6])
        at = slice(peer * SLOTS, (peer + 1) * SLOTS)
        hits_ref[:, at] = jnp.where(
            (row_at >= first_y) & (row_at <= last_y), 1.0, 0.0
        ).astype(BF16)
        cols_ref[:, at] = jnp.where(
            (col_at >= first_x) & (col_at <= last_x),
            jnp.broadcast_to(weight, col_at.shape),
            0.0,
        ).astype(BF16)
    rudy = contract(hits_ref[...], cols_ref[...], 1, 1)
    rudy = rudy + jnp.where(first_round == 0, 0.0, past_ref[...])
    rudy_ref[...] = rudy
    excess = jnp.maximum(rudy - capacity_ref[...], 0.0)

    half = 256
    lower = (iota((half, half), 0) >= iota((half, half), 1)).astype(F32).astype(BF16)
    carry = jnp.zeros((1, tile_cols), F32)
    parts = []
    for start in range(0, tile_rows, half):
        pieces = jnp.concatenate(three_parts(excess[start : start + half]), axis=1)
        sums = contract(lower, pieces, 1, 0)
        part = (
            sums[:, :tile_cols]
            + sums[:, tile_cols : 2 * tile_cols]
            + sums[:, 2 * tile_cols :]
            + carry
        )
        parts.append(part)
        carry = part[half - 1 : half, :]
    within = jnp.concatenate(parts, axis=0)
    within_ref[...] = within

    cells = bins_ref.shape[1]
    bin_row = lax.shift_right_logical(bins_ref[...], 7)
    bin_col = bins_ref[...] & 127
    area = area_ref[...]
    row_hot = jnp.where(iota((tile_rows, cells), 0) == bin_row, 1.0, 0.0).astype(BF16)
    is_col = iota((tile_cols, cells), 0) == bin_col
    turned = jnp.concatenate(three_parts(within.T), axis=0)
    picked = contract(turned, row_hot, 1, 0)
    picked = (
        picked[:tile_cols] + picked[tile_cols : 2 * tile_cols] + picked[2 * tile_cols :]
    )
    looked = jnp.sum(jnp.where(is_col, picked, 0.0), axis=0, keepdims=True)
    looked_ref[...] = looked

    high, middle, low = three_parts(area)
    pieces = jnp.concatenate(
        [high.astype(F32), middle.astype(F32), low.astype(F32), jnp.zeros((5, cells), F32)],
        axis=0,
    ).astype(BF16)
    col_area = contract(pieces, jnp.where(is_col, 1.0, 0.0).astype(BF16), 1, 1)
    col_area = jnp.sum(col_area, axis=0, keepdims=True)
    weighed = area * looked
    area_sum = area[:, :LANES]
    weighed_sum = weighed[:, :LANES]
    for k in range(1, cells // LANES):
        area_sum = area_sum + area[:, k * LANES : (k + 1) * LANES]
        weighed_sum = weighed_sum + weighed[:, k * LANES : (k + 1) * LANES]
    field = iota((8, LANES), 0)
    pay = jnp.zeros((8, LANES), F32)
    for at, row in enumerate((carry, col_area, area_sum, weighed_sum, largest)):
        pay = jnp.where(field == at, jnp.broadcast_to(row, (8, LANES)), pay)
    for peer in range(row_peers):
        pay_ref[peer] = pay


def carry_kernel(col_peers, factor, info_ref, pays_ref, carried_ref, totals_ref):
    me = info_ref[0]
    running = jnp.zeros((1, LANES), F32)
    mine = jnp.zeros((1, LANES), F32)
    area_sum = jnp.zeros((1, LANES), F32)
    weighed = jnp.zeros((1, LANES), F32)
    for peer in range(pays_ref.shape[0]):
        pay = pays_ref[peer]
        mine = jnp.where(me == peer, running, mine)
        area_sum = area_sum + pay[2:3]
        weighed = weighed + pay[3:4] + pay[1:2] * running
        running = running + pay[0:1]
    carried_ref[...] = jnp.broadcast_to(mine, carried_ref.shape)
    field = iota((8, LANES), 0)
    totals = jnp.where(
        field == 0,
        jnp.broadcast_to(area_sum, (8, LANES)),
        jnp.broadcast_to(area_sum + factor * weighed, (8, LANES)),
    )
    for peer in range(col_peers):
        totals_ref[peer] = totals


def final_kernel(
    factor,
    within_ref,
    carried_ref,
    totals_ref,
    bins_ref,
    area_ref,
    looked_ref,
    inflation_ref,
    sizes_ref,
):
    carried = carried_ref[...]
    inflation_ref[...] = 1.0 + factor * (within_ref[...] + carried[0:1])
    totals = jnp.sum(totals_ref[...], axis=0)
    area_total = jnp.sum(totals[0:1], axis=1, keepdims=True)
    grown_total = jnp.sum(totals[1:2], axis=1, keepdims=True)
    bin_col = bins_ref[...] & 127
    rows = bin_col.shape[0]
    above = jnp.take_along_axis(
        jnp.broadcast_to(carried[0:1], (rows, LANES)), bin_col, axis=1
    )
    grown = area_ref[...] * (1.0 + factor * (looked_ref[...] + above))
    sizes_ref[...] = grown * (area_total / grown_total)


def call(kernel, out_shapes, args, scratch=(), flops=1_000_000):
    smem = pl.BlockSpec(memory_space=pltpu.SMEM)
    vmem = pl.BlockSpec(memory_space=pltpu.VMEM)
    specs = [smem if a.ndim == 1 else vmem for a in args]
    return pl.pallas_call(
        kernel,
        out_shape=[jax.ShapeDtypeStruct(s, F32) for s in out_shapes],
        in_specs=specs,
        out_specs=[vmem for _ in out_shapes],
        scratch_shapes=list(scratch),
        cost_estimate=pl.CostEstimate(flops=flops, bytes_accessed=1_000_000, transcendentals=0),
    )(*args)


def exchange(payload, axis):
    return lax.all_to_all(payload, axis, 0, 0, tiled=True)


def per_device(boxes, pins, capacity, cell_bin, cell_area):
    tile_rows, tile_cols = capacity.shape
    rows, cols = lax.axis_size(ROW), lax.axis_size(COL)
    groups = lax.axis_size("col_0")
    nets = boxes.shape[1]
    cells = cell_bin.shape[1]
    factor = 2.0 / (tile_rows * rows)
    row_at = lax.axis_index(ROW)
    row_start = row_at * tile_rows
    col_start = lax.axis_index(COL) * tile_cols
    pins = pins.reshape(1, nets)

    def one_round(index, past):
        base = index * SLOTS
        (packed,) = call(
            functools.partial(
                pack_kernel, cols, groups, tile_cols * (cols // groups), tile_rows
            ),
            [(cols, 8, SLOTS)],
            (jnp.stack([row_start, base]), boxes, pins),
            [pltpu.VMEM((16, nets), F32)],
            10_000_000_000,
        )
        mine = exchange(packed, COL)
        rudy, within, looked, pay = call(
            functools.partial(tile_kernel, rows),
            [(tile_rows, tile_cols), (tile_rows, tile_cols), (1, cells), (rows, 8, LANES)],
            (jnp.stack([row_start, col_start, index]), mine, past, capacity, cell_bin, cell_area),
            [
                pltpu.VMEM((tile_rows, cols * SLOTS), BF16),
                pltpu.VMEM((tile_cols, cols * SLOTS), BF16),
            ],
            10_000_000_000,
        )
        return rudy, within, looked, exchange(pay, ROW)

    def unfinished(state):
        index, _, _, _, pays = state
        return jnp.max(pays[:, 4, 0]) > (index * SLOTS).astype(F32)

    def next_round(state):
        index, rudy, _, _, _ = state
        return (index + 1, *one_round(index, rudy))

    first = (jnp.int32(1), *one_round(jnp.int32(0), capacity))
    _, rudy, within, looked, pays = lax.while_loop(unfinished, next_round, first)

    carried, totals = call(
        functools.partial(carry_kernel, cols, factor),
        [(8, LANES), (cols, 8, LANES)],
        (row_at[None], pays),
    )
    totals = exchange(totals, COL)
    shape = (cells // LANES, LANES)
    inflation, sizes = call(
        functools.partial(final_kernel, factor),
        [(tile_rows, tile_cols), shape],
        (
            within,
            carried,
            totals,
            cell_bin.reshape(shape),
            cell_area.reshape(shape),
            looked.reshape(shape),
        ),
    )
    return rudy, inflation, sizes.reshape(cell_area.shape)


def solution(mesh):
    split = Mesh(mesh.devices.reshape(4, 2, 8, 2, 2), ROW + COL)
    placed = (P(None, COL), P(COL), P(ROW, COL), P(ROW, COL), P(ROW, COL))
    return jax.shard_map(
        per_device,
        mesh=split,
        in_specs=placed,
        out_specs=(P(ROW, COL), P(ROW, COL), P(ROW, COL)),
        check_vma=False,
    )
```

time: 263 us -> 67.3 us (0.26)
  waiting for transfers between devices: 138 us -> 15.2 us
  matrix products: 40.9 us -> 0 us
  blocking collectives: 45 us -> 15.5 us
  between operations: 15.5 us -> 0.72 us
  Pallas kernels: 0 us -> 12.3 us
  starting transfers between devices: 6.08 us -> 17.7 us
  local copies, waits for them, and re-layouts: 13.4 us -> 2.09 us
    reduce_scatter x1 -> x0, waiting for transfers between devices: 132 us -> none  [per_device(): rudy = lax.psum_scatter(band, COL, scatter_dimension=1, tiled=True)]
    psum x5 -> x0, blocking collectives: 45 us -> none  [one_axis_at_a_time(): return functools.reduce(lax.psum, axes, shard)]
    dot_general x5 -> x0, matrix products: 40.9 us -> none  [the longest x4 39.4 us: add_block(): lax.dot_general(row_hits, weighted, (((0,), (0,)), ((), ())), preferred_e...]
    all_to_all x0 -> x1, blocking collectives: none -> 15.5 us  [exchange(): return lax.all_to_all(payload, axis, 0, 0, tiled=True)]
    pallas_call x0 -> x4, Pallas kernels: none -> 12.3 us  [call(): pl.pallas_call(kernel, out_shape=[jax.ShapeDtypeStruct(s, F32) for s in o...]
    gather x1 -> x0, local copies, waits for them, and re-layouts: 11.8 us -> none  [per_device(): looked = jnp.take(inflation.reshape(-1), cell_bin[0], axis=0)]
    all_to_all x1 -> x2, starting transfers between devices: 6.04 us -> 17.7 us  [exchange(): return lax.all_to_all(payload, axis, 0, 0, tiled=True)]
    all_to_all x1 -> x2, waiting for transfers between devices: 6.45 us -> 15.2 us  [exchange(): return lax.all_to_all(payload, axis, 0, 0, tiled=True)]
  transfers between devices with their start and end apart: 2 -> 2, of which waited for: 2 -> 2; matrix products, arithmetic and copies ran while one was open for 0% -> 1% of each run, Pallas kernels for 0% -> 0%
where the time goes in v1:
time: 67.3 us; the launch traced here: 66.7 us
  starting transfers between devices  17.7 us (26%)
  blocking collectives  15.5 us (23%)
  waiting for transfers between devices  15.2 us (23%)
  Pallas kernels  12.3 us (18%)
  other arithmetic  2.56 us (4%)
  local copies, waits for them, and re-layouts  2.09 us (3%)
  between operations  0.72 us (1%)
    all_to_all x2, starting transfers between devices, exchange(): return lax.all_to_all(payload, axis, 0, 0, tiled=True)  17.7 us
    all_to_all x1, blocking collectives, exchange(): return lax.all_to_all(payload, axis, 0, 0, tiled=True)  15.5 us
    all_to_all x2, waiting for transfers between devices, exchange(): return lax.all_to_all(payload, axis, 0, 0, tiled=True)  15.2 us
    pallas_call x4, Pallas kernels, call(): pl.pallas_call(kernel, out_shape=[jax.ShapeDtypeStruct(s, F32) for s in o...  12.3 us
    unnamed x20, local copies, waits for them, and re-layouts  2.09 us
    reduce_max x1, other arithmetic, unfinished(): return jnp.max(pays[:, 4, 0]) > (index * SLOTS).astype(F32)  1.37 us
  transfers between devices with their start and end apart: 2, of which 2 were waited for; matrix products, arithmetic and copies ran while one was open for 1% of the time, Pallas kernels for 0%

profile of v1, /device:TPU:1, one launch (start us, length us, event | category | flops | bytes accessed | tf_op | source)
XLA Modules:
  0.0 66.7 jit_solution(3001761271319470795)
XLA Ops:
  0.6 0.0 copy-start.11
  0.6 0.6 pad_add_fusion.3.info_ref
  1.2 0.1 copy-done.11
  1.3 2.8 %shard_map.76 = f32[32,8,128]{2,1,0:T(8,128)} custom-call(s32[2]{0:T(128)} %pad_add_fusion.3.info_ref, s32[4,2048]{1,0:T(4,128)} %boxes_ref.1, s32[1,2048]{1,0:T(1,128)S(1)} %bitcast.23), custom_call_target="tpu_custom_call" | custom-call | flops 10000000000 | bytes 1000000 | tf_op jit(solution)/shard_map/pallas_call | solution.py:237
  4.1 0.0 copy-start.9
  4.1 11.3 %all-to-all-start.2 = ((f32[32,8,128]{2,1,0:T(8,128)}), f32[32,8,128]{2,1,0:T(8,128)S(1)}, u32[]{:S(2)}, u32[]{:S(2)}) async-start(f32[32,8,128]{2,1,0:T(8,128)} %shard_map.76), calls=%async_computation.2 | async-start | bytes 262144 | tf_op jit(solution)/shard_map/all_to_all | solution.py:248
  15.4 0.0 copy-start.7
  15.4 0.0 copy-start.6
  15.4 0.6 pad_add_fusion.2.info_ref
  16.0 8.6 %all-to-all-done.2.nets_ref = f32[32,8,128]{2,1,0:T(8,128)S(1)} async-done(((f32[32,8,128]{2,1,0:T(8,128)}), f32[32,8,128]{2,1,0:T(8,128)S(1)}, u32[]{:S(2)}, u32[]{:S(2)}) %all-to-all-start.2) | async-done | bytes 131104 | tf_op jit(solution)/shard_map/all_to_all | solution.py:248
  24.6 0.0 copy-start.5
  24.6 0.7 copy-done.5
  25.3 0.0 copy-done.9
  25.3 0.0 copy-done.7
  25.3 0.0 copy-done.6
  25.3 6.3 %shard_map.77 = (f32[512,128]{1,0:T(8,128)S(1)}, f32[512,128]{1,0:T(8,128)}, f32[1,2048]{1,0:T(1,128)}, f32[8,8,128]{2,1,0:T(8,128)}) custom-call(s32[3]{0:T(128)} %pad_add_fusion.2.info_ref, f32[32,8,128]{2,1,0:T(8,128)} %copy-done.5, f32[512,128]{1,0:T(8,128)S(1)} %copy-done.9, f32[512,128]{1,0:T(8,128)S(1)} %copy-done.9, s32[1,2048]{1,0:T(1,128)S(1)} %copy-done.6, ...), custom_call_target="tpu_custom_call" | custom-call | flops 10000000000 | bytes 1000000 | tf_op jit(solution)/shard_map/pallas_call | solution.py:237
  31.6 0.0 copy-start.10
  31.6 6.5 %all-to-all-start.3 = ((f32[8,8,128]{2,1,0:T(8,128)}), f32[8,8,128]{2,1,0:T(8,128)S(1)}, u32[]{:S(2)}, u32[]{:S(2)}) async-start(f32[8,8,128]{2,1,0:T(8,128)} %get-tuple-element.81), calls=%async_computation.3 | async-start | bytes 65536 | tf_op jit(solution)/shard_map/all_to_all | solution.py:248
  38.1 6.6 %all-to-all-done.3 = f32[8,8,128]{2,1,0:T(8,128)S(1)} async-done(((f32[8,8,128]{2,1,0:T(8,128)}), f32[8,8,128]{2,1,0:T(8,128)S(1)}, u32[]{:S(2)}, u32[]{:S(2)}) %all-to-all-start.3) | async-done | bytes 32800 | tf_op jit(solution)/shard_map/all_to_all | solution.py:248
  44.7 0.0 copy-start.3
  44.7 0.6 copy-done.3
  45.3 0.0 copy-done.10
  45.3 2.0 %while.16 = (s32[]{:T(128)}, f32[512,128]{1,0:T(8,128)S(1)}, f32[512,128]{1,0:T(8,128)}, f32[1,2048]{1,0:T(1,128)}, f32[8,8,128]{2,1,0:T(8,128)}, /*index=5*/s32...) while((s32[]{:T(128)}, f32[512,128]{1,0:T(8,128)S(1)}, ...), condition=%wide.region_1.0_spmd, body=%wide.region_0.0_spmd.sunk | while | flops 20000000000 | bytes 3671529 | solution.py:296
  45.3 1.4 %slice_reduce_fusion.1 = f32[]{:T(128)} fusion(f32[8,8,128]{2,1,0:T(8,128)} %get-tuple-element.126), kind=kLoop, calls=%fused_computation.2.clone | loop fusion | flops 7 | bytes 36 | tf_op jit(solution)/shard_map/while/cond/reduce_max | solution.py:289
  47.3 0.0 copy-start
  47.3 0.0 copy-start.2
  47.3 1.5 %shard_map.78 = (f32[8,128]{1,0:T(8,128)}, f32[32,8,128]{2,1,0:T(8,128)}) custom-call(s32[1]{0:T(128)} %bitcast.7.info_ref, f32[8,8,128]{2,1,0:T(8,128)} %get-tuple-element.84.pays_ref), custom_call_target="tpu_custom_call" | custom-call | flops 1000000 | bytes 1000000 | tf_op jit(solution)/shard_map/pallas_call | solution.py:237
  48.8 15.5 %all_to_all.27.totals_ref = f32[32,8,128]{2,1,0:T(8,128)} all-to-all(f32[32,8,128]{2,1,0:T(8,128)} %get-tuple-element.86), channel_id=1, replica_groups=mesh['row_0'=4,'row_1'=2,'col_0'=8,'col_1'=2,'col_2'=2] {'col_0','col_1'..., dimensions={0} | all-to-all | bytes 262144 | tf_op jit(solution)/shard_map/all_to_all | solution.py:248
  64.3 0.0 copy-start.8
  64.3 0.0 copy-done.2
  64.3 0.7 %copy-done.8 = f32[1,2048]{1,0:T(1,128)S(1)} copy-done((f32[1,2048]{1,0:T(1,128)S(1)}, f32[1,2048]{1,0:T(1,128)}, u32[]{:S(2)}) %copy-start.8) | copy-done | bytes 8216
  65.0 1.7 %shard_map.79 = (f32[512,128]{1,0:T(8,128)}, f32[16,128]{1,0:T(8,128)}) custom-call(f32[512,128]{1,0:T(8,128)S(1)} %copy-done.2, f32[8,128]{1,0:T(8,128)} %get-tuple-element.85.carried_ref, f32[32,8,128]{2,1,0:T(8,128)} %all_to_all.27.totals_ref, s32[16,128]{1,0:T(8,128)S(1)} %bitcast.20, f32[16,128]{1,0:T(8,128)S(1)} %bitcast.21, f32[16,128]{1,0:T(8,128)S(1)} %bitcast.22), custom_call_target="tpu_custom_call" | custom-call | flops 1000000 | bytes 1000000 | tf_op jit(solution)/shard_map/pallas_call | solution.py:237
  66.7 0.0 copy-done
Async XLA Ops:
  0.6 0.7 %copy-start.11 = (s32[2048]{0:T(1024)S(1)}, s32[2048]{0:T(1024)}, u32[]{:S(2)}) copy-start(s32[2048]{0:T(1024)} %param.8) | copy-start | bytes 24580
  4.1 21.2 %copy-start.9 = (f32[512,128]{1,0:T(8,128)S(1)}, f32[512,128]{1,0:T(8,128)}, u32[]{:S(2)}) copy-start(f32[512,128]{1,0:T(8,128)} %capacity_ref.1) | copy-start | bytes 786436
  4.1 20.5 %all-to-all-start.2 = ((f32[32,8,128]{2,1,0:T(8,128)}), f32[32,8,128]{2,1,0:T(8,128)S(1)}, u32[]{:S(2)}, u32[]{:S(2)}) async-start(f32[32,8,128]{2,1,0:T(8,128)} %shard_map.76), calls=%async_computation.2 | async-start | bytes 262144 | tf_op jit(solution)/shard_map/all_to_all | solution.py:248
  15.4 9.9 %copy-start.7 = (f32[1,2048]{1,0:T(1,128)S(1)}, f32[1,2048]{1,0:T(1,128)}, u32[]{:S(2)}) copy-start(f32[1,2048]{1,0:T(1,128)} %area_ref.1) | copy-start | bytes 24580
  15.4 9.9 %copy-start.6 = (s32[1,2048]{1,0:T(1,128)S(1)}, s32[1,2048]{1,0:T(1,128)}, u32[]{:S(2)}) copy-start(s32[1,2048]{1,0:T(1,128)} %bins_ref.1) | copy-start | bytes 24580
  24.6 0.7 copy-start.5
  31.6 13.7 %copy-start.10 = (s32[4,2048]{1,0:T(4,128)S(1)}, s32[4,2048]{1,0:T(4,128)}, u32[]{:S(2)}) copy-start(s32[4,2048]{1,0:T(4,128)} %boxes_ref.1) | copy-start | bytes 98308
  31.6 13.1 %all-to-all-start.3 = ((f32[8,8,128]{2,1,0:T(8,128)}), f32[8,8,128]{2,1,0:T(8,128)S(1)}, u32[]{:S(2)}, u32[]{:S(2)}) async-start(f32[8,8,128]{2,1,0:T(8,128)} %get-tuple-element.81), calls=%async_computation.3 | async-start | bytes 65536 | tf_op jit(solution)/shard_map/all_to_all | solution.py:248
  44.7 0.6 copy-start.3
  47.3 19.4 %copy-start = (f32[512,128]{1,0:T(8,128)}, f32[512,128]{1,0:T(8,128)S(1)}, u32[]{:S(2)}) copy-start(f32[512,128]{1,0:T(8,128)S(1)} %get-tuple-element.75) | copy-start | bytes 786436
  47.3 17.0 %copy-start.2 = (f32[512,128]{1,0:T(8,128)S(1)}, f32[512,128]{1,0:T(8,128)}, u32[]{:S(2)}) copy-start(f32[512,128]{1,0:T(8,128)} %get-tuple-element.83.within_ref) | copy-start | bytes 786436
  64.3 0.7 %copy-start.8 = (f32[1,2048]{1,0:T(1,128)S(1)}, f32[1,2048]{1,0:T(1,128)}, u32[]{:S(2)}) copy-start(f32[1,2048]{1,0:T(1,128)} %get-tuple-element.87) | copy-start | bytes 24580

commit v2 on v1

--- a/solution.py
+++ b/solution.py
@@ -34,10 +34,12 @@
     return high, middle, low
 
 
-def pack_kernel(peers, groups, group_cols, tile_rows, info_ref, boxes_ref, pins_ref, out_ref, vals_ref):
+def pack_kernel(
+    peers, groups, group_cols, tile_rows, row_ref, base_ref, boxes_ref, pins_ref, out_ref, vals_ref
+):
     nets = boxes_ref.shape[1]
-    row_start = info_ref[0]
-    base = info_ref[1]
+    row_start = row_ref[0]
+    base = base_ref[0]
     first_x, last_x = boxes_ref[0:1, :], boxes_ref[1:2, :]
     first_y, last_y = boxes_ref[2:3, :], boxes_ref[3:4, :]
     span_x = (last_x - first_x + 1).astype(F32)
@@ -86,25 +88,55 @@
             out_ref[peer] = row
 
 
+def cells_kernel(tile_rows, tile_cols, bins_ref, area_ref, row_hot_ref, col_hot_ref, sums_ref):
+    cells = bins_ref.shape[1]
+    bin_row = lax.shift_right_logical(bins_ref[...], 7)
+    bin_col = bins_ref[...] & 127
+    area = area_ref[...]
+    row_hot_ref[...] = jnp.where(iota((tile_rows, cells), 0) == bin_row, 1.0, 0.0).astype(BF16)
+    col_hot = jnp.where(iota((tile_cols, cells), 0) == bin_col, 1.0, 0.0).astype(BF16)
+    col_hot_ref[...] = col_hot
+    high, middle, low = three_parts(area)
+    pieces = jnp.concatenate(
+        [high.astype(F32), middle.astype(F32), low.astype(F32), jnp.zeros((5, cells), F32)],
+        axis=0,
+    ).astype(BF16)
+    col_area = jnp.sum(contract(pieces, col_hot, 1, 1), axis=0, keepdims=True)
+    area_sum = lane_sums(area)
+    at = iota((8, LANES), 0)
+    sums_ref[...] = jnp.where(
+        at == 0,
+        jnp.broadcast_to(col_area, (8, LANES)),
+        jnp.broadcast_to(area_sum, (8, LANES)),
+    )
+
+
+def lane_sums(row):
+    total = row[:, :LANES]
+    for k in range(1, row.shape[1] // LANES):
+        total = total + row[:, k * LANES : (k + 1) * LANES]
+    return total
+
+
 def tile_kernel(
     row_peers,
-    info_ref,
+    has_past,
+    row_ref,
+    col_ref,
     nets_ref,
-    past_ref,
     capacity_ref,
-    bins_ref,
     area_ref,
-    rudy_ref,
-    within_ref,
-    looked_ref,
-    pay_ref,
-    hits_ref,
-    cols_ref,
+    row_hot_ref,
+    col_hot_ref,
+    sums_ref,
+    *refs,
 ):
+    if has_past:
+        past_ref, *refs = refs
+    rudy_ref, within_ref, looked_ref, pay_ref, hits_ref, cols_ref = refs
     tile_rows, tile_cols = capacity_ref.shape
-    row_start = info_ref[0]
-    col_start = info_ref[1]
-    first_round = info_ref[2]
+    row_start = row_ref[0]
+    col_start = col_ref[0]
     peers = nets_ref.shape[0]
     row_at = (iota((tile_rows, SLOTS), 0) + row_start).astype(F32)
     col_at = (iota((tile_cols, SLOTS), 0) + col_start).astype(F32)
@@ -125,7 +157,8 @@
             0.0,
         ).astype(BF16)
     rudy = contract(hits_ref[...], cols_ref[...], 1, 1)
-    rudy = rudy + jnp.where(first_round == 0, 0.0, past_ref[...])
+    if has_past:
+        rudy = rudy + past_ref[...]
     rudy_ref[...] = rudy
     excess = jnp.maximum(rudy - capacity_ref[...], 0.0)
 
@@ -147,62 +180,46 @@
     within = jnp.concatenate(parts, axis=0)
     within_ref[...] = within
 
-    cells = bins_ref.shape[1]
-    bin_row = lax.shift_right_logical(bins_ref[...], 7)
-    bin_col = bins_ref[...] & 127
-    area = area_ref[...]
-    row_hot = jnp.where(iota((tile_rows, cells), 0) == bin_row, 1.0, 0.0).astype(BF16)
-    is_col = iota((tile_cols, cells), 0) == bin_col
     turned = jnp.concatenate(three_parts(within.T), axis=0)
-    picked = contract(turned, row_hot, 1, 0)
+    picked = contract(turned, row_hot_ref[...], 1, 0)
     picked = (
         picked[:tile_cols] + picked[tile_cols : 2 * tile_cols] + picked[2 * tile_cols :]
     )
-    looked = jnp.sum(jnp.where(is_col, picked, 0.0), axis=0, keepdims=True)
+    looked = jnp.sum(picked * col_hot_ref[...].astype(F32), axis=0, keepdims=True)
     looked_ref[...] = looked
-
-    high, middle, low = three_parts(area)
-    pieces = jnp.concatenate(
-        [high.astype(F32), middle.astype(F32), low.astype(F32), jnp.zeros((5, cells), F32)],
-        axis=0,
-    ).astype(BF16)
-    col_area = contract(pieces, jnp.where(is_col, 1.0, 0.0).astype(BF16), 1, 1)
-    col_area = jnp.sum(col_area, axis=0, keepdims=True)
-    weighed = area * looked
-    area_sum = area[:, :LANES]
-    weighed_sum = weighed[:, :LANES]
-    for k in range(1, cells // LANES):
-        area_sum = area_sum + area[:, k * LANES : (k + 1) * LANES]
-        weighed_sum = weighed_sum + weighed[:, k * LANES : (k + 1) * LANES]
-    field = iota((8, LANES), 0)
+    weighed_sum = lane_sums(area_ref[...] * looked)
+    at = iota((8, LANES), 0)
     pay = jnp.zeros((8, LANES), F32)
-    for at, row in enumerate((carry, col_area, area_sum, weighed_sum, largest)):
-        pay = jnp.where(field == at, jnp.broadcast_to(row, (8, LANES)), pay)
+    for k, row in enumerate((carry, sums_ref[0:1], sums_ref[1:2], weighed_sum, largest)):
+        pay = jnp.where(at == k, jnp.broadcast_to(row, (8, LANES)), pay)
     for peer in range(row_peers):
         pay_ref[peer] = pay
 
 
-def carry_kernel(col_peers, factor, info_ref, pays_ref, carried_ref, totals_ref):
-    me = info_ref[0]
+def carry_kernel(col_peers, factor, me_ref, pays_ref, carried_ref, totals_ref, most_ref):
+    me = me_ref[0]
     running = jnp.zeros((1, LANES), F32)
     mine = jnp.zeros((1, LANES), F32)
     area_sum = jnp.zeros((1, LANES), F32)
     weighed = jnp.zeros((1, LANES), F32)
+    largest = jnp.zeros((1, LANES), F32)
     for peer in range(pays_ref.shape[0]):
         pay = pays_ref[peer]
         mine = jnp.where(me == peer, running, mine)
         area_sum = area_sum + pay[2:3]
         weighed = weighed + pay[3:4] + pay[1:2] * running
+        largest = jnp.maximum(largest, pay[4:5])
         running = running + pay[0:1]
+    most_ref[0] = jnp.max(largest)
     carried_ref[...] = jnp.broadcast_to(mine, carried_ref.shape)
-    field = iota((8, LANES), 0)
-    totals = jnp.where(
-        field == 0,
-        jnp.broadcast_to(area_sum, (8, LANES)),
-        jnp.broadcast_to(area_sum + factor * weighed, (8, LANES)),
-    )
-    for peer in range(col_peers):
-        totals_ref[peer] = totals
+    grown = area_sum + factor * weighed
+    half = LANES // 2
+    both = jnp.where(
+        iota((1, LANES), 1) < half,
+        area_sum + pltpu.roll(area_sum, half, 1),
+        grown + pltpu.roll(grown, half, 1),
+    )
+    totals_ref[...] = jnp.broadcast_to(both, totals_ref.shape)
 
 
 def final_kernel(
@@ -218,9 +235,10 @@
 ):
     carried = carried_ref[...]
     inflation_ref[...] = 1.0 + factor * (within_ref[...] + carried[0:1])
-    totals = jnp.sum(totals_ref[...], axis=0)
-    area_total = jnp.sum(totals[0:1], axis=1, keepdims=True)
-    grown_total = jnp.sum(totals[1:2], axis=1, keepdims=True)
+    totals = jnp.sum(totals_ref[...], axis=0, keepdims=True)
+    lower = iota(totals.shape, 1) < LANES // 2
+    area_total = jnp.sum(jnp.where(lower, totals, 0.0), axis=1, keepdims=True)
+    grown_total = jnp.sum(jnp.where(lower, 0.0, totals), axis=1, keepdims=True)
     bin_col = bins_ref[...] & 127
     rows = bin_col.shape[0]
     above = jnp.take_along_axis(
@@ -230,16 +248,17 @@
     sizes_ref[...] = grown * (area_total / grown_total)
 
 
-def call(kernel, out_shapes, args, scratch=(), flops=1_000_000):
+def call(kernel, outs, args, scratch=(), limit=16, flops=1_000_000):
     smem = pl.BlockSpec(memory_space=pltpu.SMEM)
     vmem = pl.BlockSpec(memory_space=pltpu.VMEM)
-    specs = [smem if a.ndim == 1 else vmem for a in args]
+    outs = [o if isinstance(o, jax.ShapeDtypeStruct) else jax.ShapeDtypeStruct(o, F32) for o in outs]
     return pl.pallas_call(
         kernel,
-        out_shape=[jax.ShapeDtypeStruct(s, F32) for s in out_shapes],
-        in_specs=specs,
-        out_specs=[vmem for _ in out_shapes],
+        out_shape=outs,
+        in_specs=[smem if a.ndim == 1 else vmem for a in args],
+        out_specs=[smem if len(o.shape) == 1 else vmem for o in outs],
         scratch_shapes=list(scratch),
+        compiler_params=pltpu.CompilerParams(vmem_limit_bytes=limit * 1024 * 1024),
         cost_estimate=pl.CostEstimate(flops=flops, bytes_accessed=1_000_000, transcendentals=0),
     )(*args)
 
@@ -255,51 +274,59 @@
     nets = boxes.shape[1]
     cells = cell_bin.shape[1]
     factor = 2.0 / (tile_rows * rows)
-    row_at = lax.axis_index(ROW)
+    row_at = lax.axis_index(ROW)[None]
     row_start = row_at * tile_rows
-    col_start = lax.axis_index(COL) * tile_cols
+    col_start = lax.axis_index(COL)[None] * tile_cols
     pins = pins.reshape(1, nets)
+    row_hot, col_hot, cell_sums = call(
+        functools.partial(cells_kernel, tile_rows, tile_cols),
+        [
+            jax.ShapeDtypeStruct((tile_rows, cells), BF16),
+            jax.ShapeDtypeStruct((tile_cols, cells), BF16),
+            (8, LANES),
+        ],
+        (cell_bin, cell_area),
+        flops=4_000_000_000,
+    )
 
     def one_round(index, past):
-        base = index * SLOTS
         (packed,) = call(
             functools.partial(
                 pack_kernel, cols, groups, tile_cols * (cols // groups), tile_rows
             ),
             [(cols, 8, SLOTS)],
-            (jnp.stack([row_start, base]), boxes, pins),
+            (row_start, index[None] * SLOTS, boxes, pins),
             [pltpu.VMEM((16, nets), F32)],
-            10_000_000_000,
         )
         mine = exchange(packed, COL)
         rudy, within, looked, pay = call(
-            functools.partial(tile_kernel, rows),
+            functools.partial(tile_kernel, rows, past is not None),
             [(tile_rows, tile_cols), (tile_rows, tile_cols), (1, cells), (rows, 8, LANES)],
-            (jnp.stack([row_start, col_start, index]), mine, past, capacity, cell_bin, cell_area),
+            (row_start, col_start, mine, capacity, cell_area, row_hot, col_hot, cell_sums)
+            + (() if past is None else (past,)),
             [
                 pltpu.VMEM((tile_rows, cols * SLOTS), BF16),
                 pltpu.VMEM((tile_cols, cols * SLOTS), BF16),
             ],
-            10_000_000_000,
+            limit=28,
         )
-        return rudy, within, looked, exchange(pay, ROW)
+        carried, totals, most = call(
+            functools.partial(carry_kernel, cols, factor),
+            [(8, LANES), (cols, LANES), (1,)],
+            (row_at, exchange(pay, ROW)),
+        )
+        return index + 1, most, rudy, within, looked, carried, totals
 
     def unfinished(state):
-        index, _, _, _, pays = state
-        return jnp.max(pays[:, 4, 0]) > (index * SLOTS).astype(F32)
+        index, most, *_ = state
+        return most[0] > (index * SLOTS).astype(F32)
 
     def next_round(state):
-        index, rudy, _, _, _ = state
-        return (index + 1, *one_round(index, rudy))
-
-    first = (jnp.int32(1), *one_round(jnp.int32(0), capacity))
-    _, rudy, within, looked, pays = lax.while_loop(unfinished, next_round, first)
-
-    carried, totals = call(
-        functools.partial(carry_kernel, cols, factor),
-        [(8, LANES), (cols, 8, LANES)],
-        (row_at[None], pays),
-    )
+        return one_round(state[0], state[2])
+
+    first = one_round(jnp.int32(0), None)
+    _, _, rudy, within, looked, carried, totals = lax.while_loop(unfinished, next_round, first)
+
     totals = exchange(totals, COL)
     shape = (cells // LANES, LANES)
     inflation, sizes = call(

time: 67.3 us -> 59.5 us (0.88)
  waiting for transfers between devices: 15.2 us -> 12.6 us
  other arithmetic: 2.56 us -> 0 us
  blocking collectives: 15.5 us -> 13.3 us
  local copies, waits for them, and re-layouts: 2.09 us -> 0.71 us
  Pallas kernels: 12.3 us -> 13.6 us
    all_to_all x2, waiting for transfers between devices: 15.2 us -> 12.6 us  [exchange(): return lax.all_to_all(payload, axis, 0, 0, tiled=True)]
    all_to_all x1, blocking collectives: 15.5 us -> 13.3 us  [exchange(): return lax.all_to_all(payload, axis, 0, 0, tiled=True)]
    unnamed x20 -> x10, local copies, waits for them, and re-layouts: 2.09 us -> 0.71 us
    reduce_max x1 -> x0, other arithmetic: 1.37 us -> none  [unfinished(): return jnp.max(pays[:, 4, 0]) > (index * SLOTS).astype(F32)]
    pallas_call x4 -> x5, Pallas kernels: 12.3 us -> 13.6 us  [call(): pl.pallas_call(kernel, out_shape=outs, in_specs=[smem if a.ndim == 1 else...]
    another operation x2 -> x0, other arithmetic: 1.19 us -> none  [the longest x1 0.6 us: one_round(): jnp.stack([row_start, col_start, index])]
  transfers between devices with their start and end apart: 2 -> 2, of which waited for: 2 -> 2; matrix products, arithmetic and copies ran while one was open for 1% -> 0% of each run, Pallas kernels for 0% -> 4%
where the time goes in v2:
time: 59.5 us; the launch traced here: 59 us
  starting transfers between devices  17.5 us (29%)
  Pallas kernels  13.6 us (23%)
  blocking collectives  13.3 us (22%)
  waiting for transfers between devices  12.6 us (21%)
  local copies, waits for them, and re-layouts  0.71 us (1%)
  between operations  0.7 us (1%)
  loops' own time  0.65 us (1%)
    all_to_all x2, starting transfers between devices, exchange(): return lax.all_to_all(payload, axis, 0, 0, tiled=True)  17.5 us
    pallas_call x5, Pallas kernels, call(): pl.pallas_call(kernel, out_shape=outs, in_specs=[smem if a.ndim == 1 else...  13.6 us
    all_to_all x1, blocking collectives, exchange(): return lax.all_to_all(payload, axis, 0, 0, tiled=True)  13.3 us
    all_to_all x2, waiting for transfers between devices, exchange(): return lax.all_to_all(payload, axis, 0, 0, tiled=True)  12.6 us
  transfers between devices with their start and end apart: 2, of which 2 were waited for; matrix products, arithmetic and copies ran while one was open for 0% of the time, Pallas kernels for 4%

profile of v2, /device:TPU:1, one launch (start us, length us, event | category | flops | bytes accessed | tf_op | source)
XLA Modules:
  0.0 59.0 jit_solution(5555801189453967782)
XLA Ops:
  0.6 2.8 %shard_map.76 = f32[32,8,128]{2,1,0:T(8,128)} custom-call(s32[1]{0:T(128)} %mul.26.row_ref, s32[1]{0:T(128)} %constant.40.clone.1.base_ref, s32[4,2048]{1,0:T(4,128)} %boxes_ref.1, s32[1,2048]{1,0:T(1,128)} %bitcast.4.pins_ref), custom_call_target="tpu_custom_call" | custom-call | flops 1000000 | bytes 1000000 | tf_op jit(solution)/shard_map/pallas_call | solution.py:255
  3.4 11.1 %all-to-all-start.2 = ((f32[32,8,128]{2,1,0:T(8,128)}), f32[32,8,128]{2,1,0:T(8,128)S(1)}, u32[]{:S(2)}, u32[]{:S(2)}) async-start(f32[32,8,128]{2,1,0:T(8,128)} %shard_map.76), calls=%async_computation.2 | async-start | bytes 262144 | tf_op jit(solution)/shard_map/all_to_all | solution.py:267
  14.6 0.0 copy-start
  14.6 0.7 %copy-done = s32[1,2048]{1,0:T(1,128)S(1)} copy-done((s32[1,2048]{1,0:T(1,128)S(1)}, s32[1,2048]{1,0:T(1,128)}, u32[]{:S(2)}) %copy-start) | copy-done | bytes 8216
  15.3 0.0 copy-start.2
  15.3 0.0 copy-start.4
  15.3 2.5 %shard_map.77 = (bf16[512,2048]{1,0:T(8,128)(2,1)S(1)}, bf16[128,2048]{1,0:T(8,128)(2,1)S(1)}, f32[8,128]{1,0:T(8,128)}) custom-call(s32[1,2048]{1,0:T(1,128)S(1)} %copy-done, f32[1,2048]{1,0:T(1,128)} %area_ref.3), custom_call_target="tpu_custom_call" | custom-call | flops 4000000000 | bytes 1000000 | tf_op jit(solution)/shard_map/pallas_call | solution.py:255
  17.8 6.0 %all-to-all-done.2.nets_ref = f32[32,8,128]{2,1,0:T(8,128)S(1)} async-done(((f32[32,8,128]{2,1,0:T(8,128)}), f32[32,8,128]{2,1,0:T(8,128)S(1)}, u32[]{:S(2)}, u32[]{:S(2)}) %all-to-all-start.2) | async-done | bytes 131104 | tf_op jit(solution)/shard_map/all_to_all | solution.py:267
  23.8 0.0 copy-done.2
  23.8 0.0 copy-done.4
  23.8 5.8 %shard_map.78 = (f32[512,128]{1,0:T(8,128)S(1)}, f32[512,128]{1,0:T(8,128)}, f32[1,2048]{1,0:T(1,128)}, f32[8,8,128]{2,1,0:T(8,128)}) custom-call(s32[1]{0:T(128)} %mul.26.row_ref, s32[1]{0:T(128)} %bitcast.3.col_ref, f32[32,8,128]{2,1,0:T(8,128)S(1)} %all-to-all-done.2.nets_ref, f32[512,128]{1,0:T(8,128)S(1)} %copy-done.2, f32[1,2048]{1,0:T(1,128)S(1)} %copy-done.4, ...), custom_call_target="tpu_custom_call" | custom-call | flops 1000000 | bytes 1000000 | tf_op jit(solution)/shard_map/pallas_call | solution.py:255
  29.6 6.4 %all-to-all-start.3 = ((f32[8,8,128]{2,1,0:T(8,128)}), f32[8,8,128]{2,1,0:T(8,128)S(1)}, u32[]{:S(2)}, u32[]{:S(2)}) async-start(f32[8,8,128]{2,1,0:T(8,128)} %get-tuple-element.112), calls=%async_computation.3 | async-start | bytes 65536 | tf_op jit(solution)/shard_map/all_to_all | solution.py:267
  36.0 6.6 %all-to-all-done.3.pays_ref = f32[8,8,128]{2,1,0:T(8,128)S(1)} async-done(((f32[8,8,128]{2,1,0:T(8,128)}), f32[8,8,128]{2,1,0:T(8,128)S(1)}, u32[]{:S(2)}, u32[]{:S(2)}) %all-to-all-start.3) | async-done | bytes 32800 | tf_op jit(solution)/shard_map/all_to_all | solution.py:267
  42.6 0.7 %shard_map.79 = (f32[8,128]{1,0:T(8,128)}, f32[32,128]{1,0:T(8,128)}, f32[1]{0:T(128)}) custom-call(s32[1]{0:T(128)} %bitcast.2.me_ref, f32[8,8,128]{2,1,0:T(8,128)S(1)} %all-to-all-done.3.pays_ref), custom_call_target="tpu_custom_call" | custom-call | flops 1000000 | bytes 1000000 | tf_op jit(solution)/shard_map/pallas_call | solution.py:255
  43.3 0.0 copy-start.1
  43.3 0.6 %while.20 = (s32[]{:T(128)}, f32[1]{0:T(128)}, f32[512,128]{1,0:T(8,128)S(1)}, f32[512,128]{1,0:T(8,128)}, f32[1,2048]{1,0:T(1,128)}, /*index=5*/f32[8,128]{1,0:...) while((s32[]{:T(128)}, f32[1]{0:T(128)}, ...), condition=%wide.region_1.0_spmd, body=%wide.region_0.0_spmd.sunk | while | flops 3000005 | bytes 4016077 | solution.py:328
  44.0 0.0 copy-start.3
  44.0 13.3 %all_to_all.33 = f32[32,1,128]{2,1,0:T(1,128)S(1)} all-to-all(f32[32,1,128]{2,1,0:T(1,128)} %bitcast.17), channel_id=1, replica_groups=mesh['row_0'=4,'row_1'=2,'col_0'=8,'col_1'=2,'col_2'=2] {'col_0','col_1'..., dimensions={0} | all-to-all | bytes 32768 | tf_op jit(solution)/shard_map/all_to_all | solution.py:267
  57.3 0.0 copy-done.1
  57.3 1.7 %shard_map.80 = (f32[512,128]{1,0:T(8,128)}, f32[16,128]{1,0:T(8,128)}) custom-call(f32[512,128]{1,0:T(8,128)} %get-tuple-element.120.within_ref, f32[8,128]{1,0:T(8,128)} %get-tuple-element.121.carried_ref, f32[32,128]{1,0:T(8,128)S(1)} %bitcast.14, s32[16,128]{1,0:T(8,128)S(1)} %bitcast.15, f32[16,128]{1,0:T(8,128)S(1)} %bitcast.16, f32[16,128]{1,0:T(8,128)} %bitcast.18), custom_call_target="tpu_custom_call" | custom-call | flops 1000000 | bytes 1000000 | tf_op jit(solution)/shard_map/pallas_call | solution.py:255
  59.0 0.0 copy-done.3
Async XLA Ops:
  3.4 20.4 %all-to-all-start.2 = ((f32[32,8,128]{2,1,0:T(8,128)}), f32[32,8,128]{2,1,0:T(8,128)S(1)}, u32[]{:S(2)}, u32[]{:S(2)}) async-start(f32[32,8,128]{2,1,0:T(8,128)} %shard_map.76), calls=%async_computation.2 | async-start | bytes 262144 | tf_op jit(solution)/shard_map/all_to_all | solution.py:267
  14.6 0.7 %copy-start = (s32[1,2048]{1,0:T(1,128)S(1)}, s32[1,2048]{1,0:T(1,128)}, u32[]{:S(2)}) copy-start(s32[1,2048]{1,0:T(1,128)} %bins_ref.1) | copy-start | bytes 24580
  15.3 8.5 %copy-start.2 = (f32[512,128]{1,0:T(8,128)S(1)}, f32[512,128]{1,0:T(8,128)}, u32[]{:S(2)}) copy-start(f32[512,128]{1,0:T(8,128)} %capacity_ref.1) | copy-start | bytes 786436
  15.3 8.5 %copy-start.4 = (f32[1,2048]{1,0:T(1,128)S(1)}, f32[1,2048]{1,0:T(1,128)}, u32[]{:S(2)}) copy-start(f32[1,2048]{1,0:T(1,128)} %area_ref.3) | copy-start | bytes 24580
  29.6 12.9 %all-to-all-start.3 = ((f32[8,8,128]{2,1,0:T(8,128)}), f32[8,8,128]{2,1,0:T(8,128)S(1)}, u32[]{:S(2)}, u32[]{:S(2)}) async-start(f32[8,8,128]{2,1,0:T(8,128)} %get-tuple-element.112), calls=%async_computation.3 | async-start | bytes 65536 | tf_op jit(solution)/shard_map/all_to_all | solution.py:267
  43.3 14.0 %copy-start.1 = (s32[1,2048]{1,0:T(1,128)S(1)}, s32[1,2048]{1,0:T(1,128)}, u32[]{:S(2)}) copy-start(s32[1,2048]{1,0:T(1,128)} %bins_ref.1) | copy-start | bytes 24580
  44.0 15.0 %copy-start.3 = (f32[512,128]{1,0:T(8,128)}, f32[512,128]{1,0:T(8,128)S(1)}, u32[]{:S(2)}) copy-start(f32[512,128]{1,0:T(8,128)S(1)} %get-tuple-element.106) | copy-start | bytes 786436

commit v3 on v2

--- a/solution.py
+++ b/solution.py
@@ -88,25 +88,27 @@
             out_ref[peer] = row
 
 
-def cells_kernel(tile_rows, tile_cols, bins_ref, area_ref, row_hot_ref, col_hot_ref, sums_ref):
+def cells_kernel(tile_rows, tile_cols, bins_ref, area_ref, below_ref, sums_ref):
     cells = bins_ref.shape[1]
     bin_row = lax.shift_right_logical(bins_ref[...], 7)
     bin_col = bins_ref[...] & 127
     area = area_ref[...]
-    row_hot_ref[...] = jnp.where(iota((tile_rows, cells), 0) == bin_row, 1.0, 0.0).astype(BF16)
-    col_hot = jnp.where(iota((tile_cols, cells), 0) == bin_col, 1.0, 0.0).astype(BF16)
-    col_hot_ref[...] = col_hot
-    high, middle, low = three_parts(area)
+    reach = jnp.where(iota((tile_rows, cells), 0) <= bin_row, 1.0, 0.0).astype(BF16)
+    is_col = iota((tile_cols, cells), 0) == bin_col
     pieces = jnp.concatenate(
-        [high.astype(F32), middle.astype(F32), low.astype(F32), jnp.zeros((5, cells), F32)],
+        [jnp.where(is_col, part.astype(F32), 0.0).astype(BF16) for part in three_parts(area)],
         axis=0,
-    ).astype(BF16)
-    col_area = jnp.sum(contract(pieces, col_hot, 1, 1), axis=0, keepdims=True)
+    )
+    below = contract(reach, pieces, 1, 1)
+    below = (
+        below[:, :tile_cols] + below[:, tile_cols : 2 * tile_cols] + below[:, 2 * tile_cols :]
+    )
+    below_ref[...] = below
     area_sum = lane_sums(area)
     at = iota((8, LANES), 0)
     sums_ref[...] = jnp.where(
         at == 0,
-        jnp.broadcast_to(col_area, (8, LANES)),
+        jnp.broadcast_to(below[0:1], (8, LANES)),
         jnp.broadcast_to(area_sum, (8, LANES)),
     )
 
@@ -125,15 +127,13 @@
     col_ref,
     nets_ref,
     capacity_ref,
-    area_ref,
-    row_hot_ref,
-    col_hot_ref,
+    below_ref,
     sums_ref,
     *refs,
 ):
     if has_past:
         past_ref, *refs = refs
-    rudy_ref, within_ref, looked_ref, pay_ref, hits_ref, cols_ref = refs
+    rudy_ref, excess_ref, pay_ref, hits_ref, cols_ref = refs
     tile_rows, tile_cols = capacity_ref.shape
     row_start = row_ref[0]
     col_start = col_ref[0]
@@ -161,13 +161,25 @@
         rudy = rudy + past_ref[...]
     rudy_ref[...] = rudy
     excess = jnp.maximum(rudy - capacity_ref[...], 0.0)
-
+    excess_ref[...] = excess
+    col_sum = jnp.sum(excess, axis=0, keepdims=True)
+    weighed = jnp.sum(excess * below_ref[...], axis=0, keepdims=True)
+    at = iota((8, LANES), 0)
+    pay = jnp.zeros((8, LANES), F32)
+    for k, row in enumerate((col_sum, sums_ref[0:1], sums_ref[1:2], weighed, largest)):
+        pay = jnp.where(at == k, jnp.broadcast_to(row, (8, LANES)), pay)
+    for peer in range(row_peers):
+        pay_ref[peer] = pay
+
+
+def lookup_kernel(excess_ref, bins_ref, within_ref, looked_ref):
+    tile_rows, tile_cols = excess_ref.shape
     half = 256
     lower = (iota((half, half), 0) >= iota((half, half), 1)).astype(F32).astype(BF16)
     carry = jnp.zeros((1, tile_cols), F32)
     parts = []
     for start in range(0, tile_rows, half):
-        pieces = jnp.concatenate(three_parts(excess[start : start + half]), axis=1)
+        pieces = jnp.concatenate(three_parts(excess_ref[start : start + half]), axis=1)
         sums = contract(lower, pieces, 1, 0)
         part = (
             sums[:, :tile_cols]
@@ -180,23 +192,20 @@
     within = jnp.concatenate(parts, axis=0)
     within_ref[...] = within
 
+    cells = bins_ref.shape[1]
+    bin_row = lax.shift_right_logical(bins_ref[...], 7)
+    bin_col = bins_ref[...] & 127
+    row_hot = jnp.where(iota((tile_rows, cells), 0) == bin_row, 1.0, 0.0).astype(BF16)
     turned = jnp.concatenate(three_parts(within.T), axis=0)
-    picked = contract(turned, row_hot_ref[...], 1, 0)
+    picked = contract(turned, row_hot, 1, 0)
     picked = (
         picked[:tile_cols] + picked[tile_cols : 2 * tile_cols] + picked[2 * tile_cols :]
     )
-    looked = jnp.sum(picked * col_hot_ref[...].astype(F32), axis=0, keepdims=True)
-    looked_ref[...] = looked
-    weighed_sum = lane_sums(area_ref[...] * looked)
-    at = iota((8, LANES), 0)
-    pay = jnp.zeros((8, LANES), F32)
-    for k, row in enumerate((carry, sums_ref[0:1], sums_ref[1:2], weighed_sum, largest)):
-        pay = jnp.where(at == k, jnp.broadcast_to(row, (8, LANES)), pay)
-    for peer in range(row_peers):
-        pay_ref[peer] = pay
-
-
-def carry_kernel(col_peers, factor, me_ref, pays_ref, carried_ref, totals_ref, most_ref):
+    is_col = iota((tile_cols, cells), 0) == bin_col
+    looked_ref[...] = jnp.sum(jnp.where(is_col, picked, 0.0), axis=0, keepdims=True)
+
+
+def carry_kernel(factor, me_ref, base_ref, pays_ref, carried_ref, totals_ref, base_out, left_ref):
     me = me_ref[0]
     running = jnp.zeros((1, LANES), F32)
     mine = jnp.zeros((1, LANES), F32)
@@ -210,7 +219,8 @@
         weighed = weighed + pay[3:4] + pay[1:2] * running
         largest = jnp.maximum(largest, pay[4:5])
         running = running + pay[0:1]
-    most_ref[0] = jnp.max(largest)
+    base_out[0] = base_ref[0] + SLOTS
+    left_ref[0] = jnp.max(largest).astype(jnp.int32) - (base_ref[0] + SLOTS)
     carried_ref[...] = jnp.broadcast_to(mine, carried_ref.shape)
     grown = area_sum + factor * weighed
     half = LANES // 2
@@ -222,27 +232,18 @@
     totals_ref[...] = jnp.broadcast_to(both, totals_ref.shape)
 
 
-def final_kernel(
-    factor,
-    within_ref,
-    carried_ref,
-    totals_ref,
-    bins_ref,
-    area_ref,
-    looked_ref,
-    inflation_ref,
-    sizes_ref,
-):
-    carried = carried_ref[...]
-    inflation_ref[...] = 1.0 + factor * (within_ref[...] + carried[0:1])
+def inflation_kernel(factor, within_ref, carried_ref, inflation_ref):
+    inflation_ref[...] = 1.0 + factor * (within_ref[...] + carried_ref[0:1])
+
+
+def sizes_kernel(factor, carried_ref, totals_ref, bins_ref, area_ref, looked_ref, sizes_ref):
     totals = jnp.sum(totals_ref[...], axis=0, keepdims=True)
     lower = iota(totals.shape, 1) < LANES // 2
     area_total = jnp.sum(jnp.where(lower, totals, 0.0), axis=1, keepdims=True)
     grown_total = jnp.sum(jnp.where(lower, 0.0, totals), axis=1, keepdims=True)
     bin_col = bins_ref[...] & 127
-    rows = bin_col.shape[0]
     above = jnp.take_along_axis(
-        jnp.broadcast_to(carried[0:1], (rows, LANES)), bin_col, axis=1
+        jnp.broadcast_to(carried_ref[0:1], bin_col.shape), bin_col, axis=1
     )
     grown = area_ref[...] * (1.0 + factor * (looked_ref[...] + above))
     sizes_ref[...] = grown * (area_total / grown_total)
@@ -278,31 +279,27 @@
     row_start = row_at * tile_rows
     col_start = lax.axis_index(COL)[None] * tile_cols
     pins = pins.reshape(1, nets)
-    row_hot, col_hot, cell_sums = call(
+    below, cell_sums = call(
         functools.partial(cells_kernel, tile_rows, tile_cols),
-        [
-            jax.ShapeDtypeStruct((tile_rows, cells), BF16),
-            jax.ShapeDtypeStruct((tile_cols, cells), BF16),
-            (8, LANES),
-        ],
+        [(tile_rows, tile_cols), (8, LANES)],
         (cell_bin, cell_area),
         flops=4_000_000_000,
     )
 
-    def one_round(index, past):
+    def one_round(base, past):
         (packed,) = call(
             functools.partial(
                 pack_kernel, cols, groups, tile_cols * (cols // groups), tile_rows
             ),
             [(cols, 8, SLOTS)],
-            (row_start, index[None] * SLOTS, boxes, pins),
+            (row_start, base, boxes, pins),
             [pltpu.VMEM((16, nets), F32)],
         )
         mine = exchange(packed, COL)
-        rudy, within, looked, pay = call(
+        rudy, excess, pay = call(
             functools.partial(tile_kernel, rows, past is not None),
-            [(tile_rows, tile_cols), (tile_rows, tile_cols), (1, cells), (rows, 8, LANES)],
-            (row_start, col_start, mine, capacity, cell_area, row_hot, col_hot, cell_sums)
+            [(tile_rows, tile_cols), (tile_rows, tile_cols), (rows, 8, LANES)],
+            (row_start, col_start, mine, capacity, below, cell_sums)
             + (() if past is None else (past,)),
             [
                 pltpu.VMEM((tile_rows, cols * SLOTS), BF16),
@@ -310,36 +307,43 @@
             ],
             limit=28,
         )
-        carried, totals, most = call(
-            functools.partial(carry_kernel, cols, factor),
-            [(8, LANES), (cols, LANES), (1,)],
-            (row_at, exchange(pay, ROW)),
-        )
-        return index + 1, most, rudy, within, looked, carried, totals
+        pays = exchange(pay, ROW)
+        within, looked = call(
+            lookup_kernel,
+            [(tile_rows, tile_cols), (1, cells)],
+            (excess, cell_bin),
+            limit=28,
+            flops=4_000_000_000,
+        )
+        one = jax.ShapeDtypeStruct((1,), jnp.int32)
+        carried, totals, base, left = call(
+            functools.partial(carry_kernel, factor),
+            [(8, LANES), (cols, LANES), one, one],
+            (row_at, base, pays),
+        )
+        return left, base, rudy, within, looked, carried, totals
 
     def unfinished(state):
-        index, most, *_ = state
-        return most[0] > (index * SLOTS).astype(F32)
+        return state[0][0] > 0
 
     def next_round(state):
-        return one_round(state[0], state[2])
-
-    first = one_round(jnp.int32(0), None)
+        return one_round(state[1], state[2])
+
+    first = one_round(jnp.zeros((1,), jnp.int32), None)
     _, _, rudy, within, looked, carried, totals = lax.while_loop(unfinished, next_round, first)
 
     totals = exchange(totals, COL)
     shape = (cells // LANES, LANES)
-    inflation, sizes = call(
-        functools.partial(final_kernel, factor),
-        [(tile_rows, tile_cols), shape],
-        (
-            within,
-            carried,
-            totals,
-            cell_bin.reshape(shape),
-            cell_area.reshape(shape),
-            looked.reshape(shape),
-        ),
+    (inflation,) = call(
+        functools.partial(inflation_kernel, factor),
+        [(tile_rows, tile_cols)],
+        (within, carried),
+        flops=4_000_000_000,
+    )
+    (sizes,) = call(
+        functools.partial(sizes_kernel, factor),
+        [shape],
+        (carried, totals, cell_bin.reshape(shape), cell_area.reshape(shape), looked.reshape(shape)),
     )
     return rudy, inflation, sizes.reshape(cell_area.shape)
 

time: 59.5 us -> 56.1 us (0.943)
  blocking collectives: 13.3 us -> 0 us
  waiting for transfers between devices: 12.6 us -> 18.8 us
  starting transfers between devices: 17.5 us -> 23.1 us
  Pallas kernels: 13.6 us -> 11.7 us
    all_to_all x1 -> x0, blocking collectives: 13.3 us -> none  [exchange(): return lax.all_to_all(payload, axis, 0, 0, tiled=True)]
    all_to_all x2 -> x3, waiting for transfers between devices: 12.6 us -> 18.8 us  [exchange(): return lax.all_to_all(payload, axis, 0, 0, tiled=True)]
    all_to_all x2 -> x3, starting transfers between devices: 17.5 us -> 23.1 us  [exchange(): return lax.all_to_all(payload, axis, 0, 0, tiled=True)]
    pallas_call x5 -> x7, Pallas kernels: 13.6 us -> 11.7 us  [call(): pl.pallas_call(kernel, out_shape=outs, in_specs=[smem if a.ndim == 1 else...]
  transfers between devices with their start and end apart: 2 -> 3, of which waited for: 2 -> 3; matrix products, arithmetic and copies ran while one was open for 0% -> 0% of each run, Pallas kernels for 4% -> 9%
where the time goes in v3:
time: 56.1 us; the launch traced here: 55.6 us
  starting transfers between devices  23.1 us (41%)
  waiting for transfers between devices  18.8 us (34%)
  Pallas kernels  11.7 us (21%)
  local copies, waits for them, and re-layouts  0.76 us (1%)
  between operations  0.75 us (1%)
    all_to_all x3, starting transfers between devices, exchange(): return lax.all_to_all(payload, axis, 0, 0, tiled=True)  23.1 us
    all_to_all x3, waiting for transfers between devices, exchange(): return lax.all_to_all(payload, axis, 0, 0, tiled=True)  18.8 us
    pallas_call x7, Pallas kernels, call(): pl.pallas_call(kernel, out_shape=outs, in_specs=[smem if a.ndim == 1 else...  11.7 us
  transfers between devices with their start and end apart: 3, of which 3 were waited for; matrix products, arithmetic and copies ran while one was open for 0% of the time, Pallas kernels for 9%

profile of v3, /device:TPU:1, one launch (start us, length us, event | category | flops | bytes accessed | tf_op | source)
XLA Modules:
  0.0 55.6 jit_solution(5031196215067063068)
XLA Ops:
  0.6 0.0 copy-start.3
  0.6 0.0 copy-start.4
  0.7 0.7 %copy-done.3 = s32[4,2048]{1,0:T(4,128)S(1)} copy-done((s32[4,2048]{1,0:T(4,128)S(1)}, s32[4,2048]{1,0:T(4,128)}, u32[]{:S(2)}) %copy-start.3) | copy-done | bytes 32792
  1.4 0.0 copy-done.4
  1.4 2.0 %shard_map.76 = f32[32,8,128]{2,1,0:T(8,128)} custom-call(s32[1]{0:T(128)} %mul.18.row_ref, s32[1]{0:T(128)} %constant.29.clone.1.base_ref, s32[4,2048]{1,0:T(4,128)S(1)} %copy-done.3, s32[1,2048]{1,0:T(1,128)S(1)} %bitcast.12), custom_call_target="tpu_custom_call" | custom-call | flops 1000000 | bytes 1000000 | tf_op jit(solution)/shard_map/pallas_call | solution.py:256
  3.4 0.0 copy-start
  3.4 0.0 copy-start.5
  3.4 11.3 %all-to-all-start.2 = ((f32[32,8,128]{2,1,0:T(8,128)}), f32[32,8,128]{2,1,0:T(8,128)S(1)}, u32[]{:S(2)}, u32[]{:S(2)}) async-start(f32[32,8,128]{2,1,0:T(8,128)} %shard_map.76), calls=%async_computation.2 | async-start | bytes 262144 | tf_op jit(solution)/shard_map/all_to_all | solution.py:268
  14.7 0.0 copy-done
  14.7 0.0 copy-done.5
  14.7 0.0 copy-start.1
  14.7 1.3 %shard_map.77 = (f32[512,128]{1,0:T(8,128)S(1)}, f32[8,128]{1,0:T(8,128)S(1)}) custom-call(s32[1,2048]{1,0:T(1,128)S(1)} %copy-done.5, f32[1,2048]{1,0:T(1,128)S(1)} %copy-done), custom_call_target="tpu_custom_call" | custom-call | flops 4000000000 | bytes 1000000 | tf_op jit(solution)/shard_map/pallas_call | solution.py:256
  16.0 7.9 %all-to-all-done.2.nets_ref = f32[32,8,128]{2,1,0:T(8,128)S(1)} async-done(((f32[32,8,128]{2,1,0:T(8,128)}), f32[32,8,128]{2,1,0:T(8,128)S(1)}, u32[]{:S(2)}, u32[]{:S(2)}) %all-to-all-start.2) | async-done | bytes 131104 | tf_op jit(solution)/shard_map/all_to_all | solution.py:268
  23.9 0.0 copy-done.1
  23.9 3.3 %shard_map.78 = (f32[512,128]{1,0:T(8,128)S(1)}, f32[512,128]{1,0:T(8,128)S(1)}, f32[8,8,128]{2,1,0:T(8,128)}) custom-call(s32[1]{0:T(128)} %mul.18.row_ref, s32[1]{0:T(128)} %bitcast.2.col_ref, f32[32,8,128]{2,1,0:T(8,128)S(1)} %all-to-all-done.2.nets_ref, f32[512,128]{1,0:T(8,128)S(1)} %copy-done.1, f32[512,128]{1,0:T(8,128)S(1)} %get-tuple-element.180.below_ref, ...), custom_call_target="tpu_custom_call" | custom-call | flops 1000000 | bytes 1000000 | tf_op jit(solution)/shard_map/pallas_call | solution.py:256
  27.2 6.4 %all-to-all-start.3 = ((f32[8,8,128]{2,1,0:T(8,128)}), f32[8,8,128]{2,1,0:T(8,128)S(1)}, u32[]{:S(2)}, u32[]{:S(2)}) async-start(f32[8,8,128]{2,1,0:T(8,128)} %get-tuple-element.106), calls=%async_computation.3 | async-start | bytes 65536 | tf_op jit(solution)/shard_map/all_to_all | solution.py:268
  33.6 2.0 %shard_map.80 = (f32[512,128]{1,0:T(8,128)}, f32[1,2048]{1,0:T(1,128)}) custom-call(f32[512,128]{1,0:T(8,128)S(1)} %get-tuple-element.110.excess_ref, s32[1,2048]{1,0:T(1,128)S(1)} %copy-done.5), custom_call_target="tpu_custom_call" | custom-call | flops 4000000000 | bytes 1000000 | tf_op jit(solution)/shard_map/pallas_call | solution.py:256
  35.6 4.6 %all-to-all-done.3.pays_ref = f32[8,8,128]{2,1,0:T(8,128)S(1)} async-done(((f32[8,8,128]{2,1,0:T(8,128)}), f32[8,8,128]{2,1,0:T(8,128)S(1)}, u32[]{:S(2)}, u32[]{:S(2)}) %all-to-all-start.3) | async-done | bytes 32800 | tf_op jit(solution)/shard_map/all_to_all | solution.py:268
  40.2 0.7 %shard_map.79 = (f32[8,128]{1,0:T(8,128)}, f32[32,128]{1,0:T(8,128)}, s32[1]{0:T(128)}, s32[1]{0:T(128)}) custom-call(s32[1]{0:T(128)} %bitcast.1.me_ref, s32[1]{0:T(128)} %constant.29.clone.1.base_ref, f32[8,8,128]{2,1,0:T(8,128)S(1)} %all-to-all-done.3.pays_ref), custom_call_target="tpu_custom_call" | custom-call | flops 1000000 | bytes 1000000 | tf_op jit(solution)/shard_map/pallas_call | solution.py:256
  40.9 0.6 while.19
  41.4 0.0 copy-start.2
  41.4 0.0 copy-start.7
  41.4 5.5 %all-to-all-start.4 = ((f32[32,1,128]{2,1,0:T(1,128)}), f32[32,1,128]{2,1,0:T(1,128)S(1)}, u32[]{:S(2)}, u32[]{:S(2)}) async-start(f32[32,1,128]{2,1,0:T(1,128)} %bitcast.14), calls=%async_computation.4 | async-start | bytes 32768 | tf_op jit(solution)/shard_map/all_to_all | solution.py:268
  46.9 0.0 copy-done.7
  46.9 1.7 %shard_map.81 = f32[512,128]{1,0:T(8,128)} custom-call(f32[512,128]{1,0:T(8,128)} %get-tuple-element.116.within_ref, f32[8,128]{1,0:T(8,128)S(1)} %copy-done.7), custom_call_target="tpu_custom_call" | custom-call | flops 4000000000 | bytes 1000000 | tf_op jit(solution)/shard_map/pallas_call | solution.py:256
  48.6 0.0 copy-done.2
  48.6 0.0 copy-start.6
  48.6 6.3 %all-to-all-done.4 = f32[32,1,128]{2,1,0:T(1,128)S(1)} async-done(((f32[32,1,128]{2,1,0:T(1,128)}), f32[32,1,128]{2,1,0:T(1,128)S(1)}, u32[]{:S(2)}, u32[]{:S(2)}) %all-to-all-start.4) | async-done | bytes 16416 | tf_op jit(solution)/shard_map/all_to_all | solution.py:268
  54.9 0.0 copy-done.6
  54.9 0.7 %shard_map.82 = f32[16,128]{1,0:T(8,128)} custom-call(f32[8,128]{1,0:T(8,128)S(1)} %copy-done.7, f32[32,128]{1,0:T(8,128)S(1)} %bitcast.10, s32[16,128]{1,0:T(8,128)S(1)} %bitcast.15, f32[16,128]{1,0:T(8,128)S(1)} %bitcast.11, f32[16,128]{1,0:T(8,128)S(1)} %bitcast.16), custom_call_target="tpu_custom_call" | custom-call | flops 1000000 | bytes 1000000 | tf_op jit(solution)/shard_map/pallas_call | solution.py:256
Async XLA Ops:
  0.6 0.8 %copy-start.3 = (s32[4,2048]{1,0:T(4,128)S(1)}, s32[4,2048]{1,0:T(4,128)}, u32[]{:S(2)}) copy-start(s32[4,2048]{1,0:T(4,128)} %boxes_ref.1) | copy-start | bytes 98308
  0.6 0.7 %copy-start.4 = (s32[2048]{0:T(1024)S(1)}, s32[2048]{0:T(1024)}, u32[]{:S(2)}) copy-start(s32[2048]{0:T(1024)} %param.8) | copy-start | bytes 24580
  3.4 11.3 %copy-start = (f32[1,2048]{1,0:T(1,128)S(1)}, f32[1,2048]{1,0:T(1,128)}, u32[]{:S(2)}) copy-start(f32[1,2048]{1,0:T(1,128)} %area_ref.1) | copy-start | bytes 24580
  3.4 11.3 %copy-start.5 = (s32[1,2048]{1,0:T(1,128)S(1)}, s32[1,2048]{1,0:T(1,128)}, u32[]{:S(2)}) copy-start(s32[1,2048]{1,0:T(1,128)} %bins_ref.3) | copy-start | bytes 24580
  3.4 20.5 %all-to-all-start.2 = ((f32[32,8,128]{2,1,0:T(8,128)}), f32[32,8,128]{2,1,0:T(8,128)S(1)}, u32[]{:S(2)}, u32[]{:S(2)}) async-start(f32[32,8,128]{2,1,0:T(8,128)} %shard_map.76), calls=%async_computation.2 | async-start | bytes 262144 | tf_op jit(solution)/shard_map/all_to_all | solution.py:268
  14.7 9.2 %copy-start.1 = (f32[512,128]{1,0:T(8,128)S(1)}, f32[512,128]{1,0:T(8,128)}, u32[]{:S(2)}) copy-start(f32[512,128]{1,0:T(8,128)} %capacity_ref.1) | copy-start | bytes 786436
  27.2 12.9 %all-to-all-start.3 = ((f32[8,8,128]{2,1,0:T(8,128)}), f32[8,8,128]{2,1,0:T(8,128)S(1)}, u32[]{:S(2)}, u32[]{:S(2)}) async-start(f32[8,8,128]{2,1,0:T(8,128)} %get-tuple-element.106), calls=%async_computation.3 | async-start | bytes 65536 | tf_op jit(solution)/shard_map/all_to_all | solution.py:268
  41.4 7.2 %copy-start.2 = (f32[512,128]{1,0:T(8,128)}, f32[512,128]{1,0:T(8,128)S(1)}, u32[]{:S(2)}) copy-start(f32[512,128]{1,0:T(8,128)S(1)} %get-tuple-element.101) | copy-start | bytes 786436
  41.4 5.5 %copy-start.7 = (f32[8,128]{1,0:T(8,128)S(1)}, f32[8,128]{1,0:T(8,128)}, u32[]{:S(2)}) copy-start(f32[8,128]{1,0:T(8,128)} %get-tuple-element.117.carried_ref) | copy-start | bytes 12292
  41.4 13.5 %all-to-all-start.4 = ((f32[32,1,128]{2,1,0:T(1,128)}), f32[32,1,128]{2,1,0:T(1,128)S(1)}, u32[]{:S(2)}, u32[]{:S(2)}) async-start(f32[32,1,128]{2,1,0:T(1,128)} %bitcast.14), calls=%async_computation.4 | async-start | bytes 32768 | tf_op jit(solution)/shard_map/all_to_all | solution.py:268
  48.6 6.3 %copy-start.6 = (f32[1,2048]{1,0:T(1,128)S(1)}, f32[1,2048]{1,0:T(1,128)}, u32[]{:S(2)}) copy-start(f32[1,2048]{1,0:T(1,128)} %get-tuple-element.119) | copy-start | bytes 24580

commit v4 on v3

--- a/solution.py
+++ b/solution.py
@@ -10,6 +10,7 @@
 
 ROW = ("row_0", "row_1")
 COL = ("col_0", "col_1", "col_2")
+NEAR = ("row_0", "row_1", "col_1", "col_2")
 SLOTS = 128
 LANES = 128
 F32 = jnp.float32
@@ -74,13 +75,16 @@
         ranks.append(before[rows] + offset)
         offset = offset + whole[rows]
     rank = jnp.concatenate(ranks, axis=1)
-    rank = jnp.where(hit > 0.0, rank - base.astype(F32), -1.0)
+    rank = jnp.clip(rank - base.astype(F32), -1.0, float(SLOTS))
+    rank = jnp.where(hit > 0.0, rank, -1.0)
     largest = jnp.max(offset, axis=0, keepdims=True)
 
-    slot = iota((SLOTS, nets), 0).astype(F32)
+    slot = iota((SLOTS, nets), 0).astype(F32).astype(BF16)
     field = iota((8, SLOTS), 0)
     for group in range(groups):
-        chosen = jnp.where(slot == rank[group : group + 1, :], 1.0, 0.0).astype(BF16)
+        mine = jnp.broadcast_to(rank[group : group + 1, :], (16, nets)).astype(BF16)
+        mine = jnp.concatenate([mine] * (SLOTS // 16), axis=0)
+        chosen = jnp.where(slot == mine, BF16(1), BF16(0))
         got = contract(vals, chosen, 1, 1)
         row = got[0:8] * 256.0 + got[8:16]
         row = jnp.where(field == 5, jnp.broadcast_to(largest, (8, SLOTS)), row)
@@ -120,8 +124,18 @@
     return total
 
 
+def tall(row, rows):
+    short = jnp.broadcast_to(row, (16, row.shape[1])).astype(BF16)
+    return jnp.concatenate([short] * (rows // 16), axis=0)
+
+
+def inside(first, last, start, count):
+    first = jnp.clip(first - start, 0.0, float(count))
+    last = jnp.clip(last - start, -1.0, float(count - 1))
+    return tall(first, count), tall(last, count)
+
+
 def tile_kernel(
-    row_peers,
     has_past,
     row_ref,
     col_ref,
@@ -133,30 +147,37 @@
 ):
     if has_past:
         past_ref, *refs = refs
-    rudy_ref, excess_ref, pay_ref, hits_ref, cols_ref = refs
+    rudy_ref, excess_ref, pay_ref = refs
     tile_rows, tile_cols = capacity_ref.shape
     row_start = row_ref[0]
     col_start = col_ref[0]
     peers = nets_ref.shape[0]
-    row_at = (iota((tile_rows, SLOTS), 0) + row_start).astype(F32)
-    col_at = (iota((tile_cols, SLOTS), 0) + col_start).astype(F32)
+    half = 256
+    at = iota((half, SLOTS), 0).astype(F32).astype(BF16)
+    col_at = at[:tile_cols]
     largest = jnp.zeros((1, SLOTS), F32)
-    for peer in range(peers):
-        box = nets_ref[peer]
-        first_x, last_x = box[0:1], box[1:2]
-        first_y, last_y = box[2:3], box[3:4]
-        weight = box[4:5]
-        largest = jnp.maximum(largest, box[5:6])
-        at = slice(peer * SLOTS, (peer + 1) * SLOTS)
-        hits_ref[:, at] = jnp.where(
-            (row_at >= first_y) & (row_at <= last_y), 1.0, 0.0
-        ).astype(BF16)
-        cols_ref[:, at] = jnp.where(
-            (col_at >= first_x) & (col_at <= last_x),
-            jnp.broadcast_to(weight, col_at.shape),
-            0.0,
-        ).astype(BF16)
-    rudy = contract(hits_ref[...], cols_ref[...], 1, 1)
+    starts = [col_start.astype(F32)] + [
+        (row_start + first).astype(F32) for first in range(0, tile_rows, half)
+    ]
+    rudy = jnp.zeros((tile_rows, tile_cols), F32)
+    step = 4
+    for peer in range(0, peers, step):
+        hits, cols = [], []
+        for box in [nets_ref[peer + k] for k in range(step)]:
+            largest = jnp.maximum(largest, box[5:6])
+            hit = []
+            for first in starts[1:]:
+                low, high = inside(box[2:3], box[3:4], first, half)
+                hit.append(
+                    jnp.where((at >= low) & (at <= high), BF16(1), BF16(0))
+                )
+            hits.append(jnp.concatenate(hit, axis=0))
+            low, high = inside(box[0:1], box[1:2], starts[0], tile_cols)
+            weight = tall(box[4:5], tile_cols)
+            cols.append(jnp.where((col_at >= low) & (col_at <= high), weight, BF16(0)))
+        rudy = rudy + contract(
+            jnp.concatenate(hits, axis=1), jnp.concatenate(cols, axis=1), 1, 1
+        )
     if has_past:
         rudy = rudy + past_ref[...]
     rudy_ref[...] = rudy
@@ -164,12 +185,19 @@
     excess_ref[...] = excess
     col_sum = jnp.sum(excess, axis=0, keepdims=True)
     weighed = jnp.sum(excess * below_ref[...], axis=0, keepdims=True)
-    at = iota((8, LANES), 0)
-    pay = jnp.zeros((8, LANES), F32)
-    for k, row in enumerate((col_sum, sums_ref[0:1], sums_ref[1:2], weighed, largest)):
+    at = iota((8, LANES), 0) & 3
+    shared = halves(sums_ref[1:2], weighed)
+    pay = jnp.broadcast_to(largest, (8, LANES))
+    for k, row in enumerate((col_sum, sums_ref[0:1], shared)):
         pay = jnp.where(at == k, jnp.broadcast_to(row, (8, LANES)), pay)
-    for peer in range(row_peers):
-        pay_ref[peer] = pay
+    for k in range(pay_ref.shape[0] // 8):
+        pay_ref[8 * k : 8 * k + 8] = pay
+
+
+def halves(a, b):
+    half = LANES // 2
+    lower = iota((1, LANES), 1) < half
+    return jnp.where(lower, a + pltpu.roll(a, half, 1), b + pltpu.roll(b, half, 1))
 
 
 def lookup_kernel(excess_ref, bins_ref, within_ref, looked_ref):
@@ -205,31 +233,30 @@
     looked_ref[...] = jnp.sum(jnp.where(is_col, picked, 0.0), axis=0, keepdims=True)
 
 
-def carry_kernel(factor, me_ref, base_ref, pays_ref, carried_ref, totals_ref, base_out, left_ref):
-    me = me_ref[0]
-    running = jnp.zeros((1, LANES), F32)
+def carry_kernel(
+    rows, factor, row_ref, col_ref, base_ref, pays_ref, carried_ref, totals_ref, base_out, left_ref
+):
+    row_me, col_me = row_ref[0], col_ref[0]
+    width = pays_ref.shape[0] // (4 * rows)
     mine = jnp.zeros((1, LANES), F32)
-    area_sum = jnp.zeros((1, LANES), F32)
-    weighed = jnp.zeros((1, LANES), F32)
+    bilinear = jnp.zeros((1, LANES), F32)
+    shared = jnp.zeros((1, LANES), F32)
     largest = jnp.zeros((1, LANES), F32)
-    for peer in range(pays_ref.shape[0]):
-        pay = pays_ref[peer]
-        mine = jnp.where(me == peer, running, mine)
-        area_sum = area_sum + pay[2:3]
-        weighed = weighed + pay[3:4] + pay[1:2] * running
-        largest = jnp.maximum(largest, pay[4:5])
-        running = running + pay[0:1]
+    for col in range(width):
+        running = jnp.zeros((1, LANES), F32)
+        for row in range(rows):
+            at = 4 * (row * width + col)
+            pay = pays_ref[at : at + 4]
+            mine = jnp.where((row_me == row) & (col_me == col), running, mine)
+            bilinear = bilinear + pay[1:2] * running
+            shared = shared + pay[2:3]
+            largest = jnp.maximum(largest, pay[3:4])
+            running = running + pay[0:1]
     base_out[0] = base_ref[0] + SLOTS
     left_ref[0] = jnp.max(largest).astype(jnp.int32) - (base_ref[0] + SLOTS)
     carried_ref[...] = jnp.broadcast_to(mine, carried_ref.shape)
-    grown = area_sum + factor * weighed
-    half = LANES // 2
-    both = jnp.where(
-        iota((1, LANES), 1) < half,
-        area_sum + pltpu.roll(area_sum, half, 1),
-        grown + pltpu.roll(grown, half, 1),
-    )
-    totals_ref[...] = jnp.broadcast_to(both, totals_ref.shape)
+    totals = shared + halves(jnp.zeros((1, LANES), F32), bilinear)
+    totals_ref[...] = jnp.broadcast_to(totals, totals_ref.shape)
 
 
 def inflation_kernel(factor, within_ref, carried_ref, inflation_ref):
@@ -240,7 +267,8 @@
     totals = jnp.sum(totals_ref[...], axis=0, keepdims=True)
     lower = iota(totals.shape, 1) < LANES // 2
     area_total = jnp.sum(jnp.where(lower, totals, 0.0), axis=1, keepdims=True)
-    grown_total = jnp.sum(jnp.where(lower, 0.0, totals), axis=1, keepdims=True)
+    added = jnp.sum(jnp.where(lower, 0.0, totals), axis=1, keepdims=True)
+    grown_total = area_total + factor * added
     bin_col = bins_ref[...] & 127
     above = jnp.take_along_axis(
         jnp.broadcast_to(carried_ref[0:1], bin_col.shape), bin_col, axis=1
@@ -276,6 +304,8 @@
     cells = cell_bin.shape[1]
     factor = 2.0 / (tile_rows * rows)
     row_at = lax.axis_index(ROW)[None]
+    near = lax.axis_size(NEAR)
+    near_at = lax.axis_index(("col_1", "col_2"))[None]
     row_start = row_at * tile_rows
     col_start = lax.axis_index(COL)[None] * tile_cols
     pins = pins.reshape(1, nets)
@@ -297,17 +327,13 @@
         )
         mine = exchange(packed, COL)
         rudy, excess, pay = call(
-            functools.partial(tile_kernel, rows, past is not None),
-            [(tile_rows, tile_cols), (tile_rows, tile_cols), (rows, 8, LANES)],
+            functools.partial(tile_kernel, past is not None),
+            [(tile_rows, tile_cols), (tile_rows, tile_cols), (near * 4, LANES)],
             (row_start, col_start, mine, capacity, below, cell_sums)
             + (() if past is None else (past,)),
-            [
-                pltpu.VMEM((tile_rows, cols * SLOTS), BF16),
-                pltpu.VMEM((tile_cols, cols * SLOTS), BF16),
-            ],
             limit=28,
         )
-        pays = exchange(pay, ROW)
+        pays = exchange(pay.reshape(near, 4, LANES), NEAR).reshape(near * 4, LANES)
         within, looked = call(
             lookup_kernel,
             [(tile_rows, tile_cols), (1, cells)],
@@ -317,9 +343,9 @@
         )
         one = jax.ShapeDtypeStruct((1,), jnp.int32)
         carried, totals, base, left = call(
-            functools.partial(carry_kernel, factor),
-            [(8, LANES), (cols, LANES), one, one],
-            (row_at, base, pays),
+            functools.partial(carry_kernel, rows, factor),
+            [(8, LANES), (groups, LANES), one, one],
+            (row_at, near_at, base, pays),
         )
         return left, base, rudy, within, looked, carried, totals
 
@@ -332,7 +358,7 @@
     first = one_round(jnp.zeros((1,), jnp.int32), None)
     _, _, rudy, within, looked, carried, totals = lax.while_loop(unfinished, next_round, first)
 
-    totals = exchange(totals, COL)
+    totals = exchange(totals, "col_0")
     shape = (cells // LANES, LANES)
     (inflation,) = call(
         functools.partial(inflation_kernel, factor),

time: 56.1 us -> 53.1 us (0.947)
  Pallas kernels: 11.7 us -> 10.4 us
  starting transfers between devices: 23.1 us -> 22 us
  waiting for transfers between devices: 18.8 us -> 18.1 us
    pallas_call x7, Pallas kernels: 11.7 us -> 10.4 us  [call(): pl.pallas_call(kernel, out_shape=outs, in_specs=[smem if a.ndim == 1 else...]
    all_to_all x3, starting transfers between devices: 23.1 us -> 22 us  [exchange(): return lax.all_to_all(payload, axis, 0, 0, tiled=True)]
    all_to_all x3, waiting for transfers between devices: 18.8 us -> 18.1 us  [exchange(): return lax.all_to_all(payload, axis, 0, 0, tiled=True)]
where the time goes in v4:
time: 53.1 us; the launch traced here: 52.6 us
  starting transfers between devices  22 us (41%)
  waiting for transfers between devices  18.1 us (34%)
  Pallas kernels  10.4 us (20%)
  local copies, waits for them, and re-layouts  0.76 us (1%)
  between operations  0.76 us (1%)
  loops' own time  0.64 us (1%)
    all_to_all x3, starting transfers between devices, exchange(): return lax.all_to_all(payload, axis, 0, 0, tiled=True)  22 us
    all_to_all x3, waiting for transfers between devices, exchange(): return lax.all_to_all(payload, axis, 0, 0, tiled=True)  18.1 us
    pallas_call x7, Pallas kernels, call(): pl.pallas_call(kernel, out_shape=outs, in_specs=[smem if a.ndim == 1 else...  10.4 us
  transfers between devices with their start and end apart: 3, of which 3 were waited for; matrix products, arithmetic and copies ran while one was open for 0% of the time, Pallas kernels for 9%

profile of v4, /device:TPU:1, one launch (start us, length us, event | category | flops | bytes accessed | tf_op | source)
XLA Modules:
  0.0 52.6 jit_solution(8590735882262590628)
XLA Ops:
  0.6 0.0 copy-start.3
  0.6 0.0 copy-start.4
  0.7 0.7 %copy-done.3 = s32[4,2048]{1,0:T(4,128)S(1)} copy-done((s32[4,2048]{1,0:T(4,128)S(1)}, s32[4,2048]{1,0:T(4,128)}, u32[]{:S(2)}) %copy-start.3) | copy-done | bytes 32792
  1.4 0.0 copy-done.4
  1.4 2.0 %shard_map.76 = f32[32,8,128]{2,1,0:T(8,128)} custom-call(s32[1]{0:T(128)} %mul.20.row_ref, s32[1]{0:T(128)} %constant.29.clone.1.base_ref, s32[4,2048]{1,0:T(4,128)S(1)} %copy-done.3, s32[1,2048]{1,0:T(1,128)S(1)} %bitcast.19), custom_call_target="tpu_custom_call" | custom-call | flops 1000000 | bytes 1000000 | tf_op jit(solution)/shard_map/pallas_call | solution.py:284
  3.4 0.0 copy-start
  3.4 0.0 copy-start.5
  3.4 11.3 %all-to-all-start.2 = ((f32[32,8,128]{2,1,0:T(8,128)}), f32[32,8,128]{2,1,0:T(8,128)S(1)}, u32[]{:S(2)}, u32[]{:S(2)}) async-start(f32[32,8,128]{2,1,0:T(8,128)} %shard_map.76), calls=%async_computation.2 | async-start | bytes 262144 | tf_op jit(solution)/shard_map/all_to_all | solution.py:296
  14.7 0.0 copy-done
  14.7 0.0 copy-done.5
  14.7 0.0 copy-start.1
  14.7 1.3 %shard_map.77 = (f32[512,128]{1,0:T(8,128)S(1)}, f32[8,128]{1,0:T(8,128)S(1)}) custom-call(s32[1,2048]{1,0:T(1,128)S(1)} %copy-done.5, f32[1,2048]{1,0:T(1,128)S(1)} %copy-done), custom_call_target="tpu_custom_call" | custom-call | flops 4000000000 | bytes 1000000 | tf_op jit(solution)/shard_map/pallas_call | solution.py:284
  16.0 7.9 %all-to-all-done.2.nets_ref = f32[32,8,128]{2,1,0:T(8,128)S(1)} async-done(((f32[32,8,128]{2,1,0:T(8,128)}), f32[32,8,128]{2,1,0:T(8,128)S(1)}, u32[]{:S(2)}, u32[]{:S(2)}) %all-to-all-start.2) | async-done | bytes 131104 | tf_op jit(solution)/shard_map/all_to_all | solution.py:296
  23.9 0.0 copy-done.1
  23.9 2.0 %shard_map.78 = (f32[512,128]{1,0:T(8,128)S(1)}, f32[512,128]{1,0:T(8,128)S(1)}, f32[128,128]{1,0:T(8,128)}) custom-call(s32[1]{0:T(128)} %mul.20.row_ref, s32[1]{0:T(128)} %bitcast.5.col_ref, f32[32,8,128]{2,1,0:T(8,128)S(1)} %all-to-all-done.2.nets_ref, f32[512,128]{1,0:T(8,128)S(1)} %copy-done.1, f32[512,128]{1,0:T(8,128)S(1)} %get-tuple-element.188.below_ref, ...), custom_call_target="tpu_custom_call" | custom-call | flops 1000000 | bytes 1000000 | tf_op jit(solution)/shard_map/pallas_call | solution.py:284
  25.9 7.4 %all-to-all-start.3 = ((f32[32,4,128]{2,1,0:T(4,128)}), f32[32,4,128]{2,1,0:T(4,128)S(1)}, u32[]{:S(2)}, u32[]{:S(2)}) async-start(f32[32,4,128]{2,1,0:T(4,128)} %bitcast.7), calls=%async_computation.3 | async-start | bytes 131072 | tf_op jit(solution)/shard_map/all_to_all | solution.py:296
  33.3 2.0 %shard_map.80 = (f32[512,128]{1,0:T(8,128)}, f32[1,2048]{1,0:T(1,128)}) custom-call(f32[512,128]{1,0:T(8,128)S(1)} %get-tuple-element.115.excess_ref, s32[1,2048]{1,0:T(1,128)S(1)} %copy-done.5), custom_call_target="tpu_custom_call" | custom-call | flops 4000000000 | bytes 1000000 | tf_op jit(solution)/shard_map/pallas_call | solution.py:284
  35.3 5.4 %all-to-all-done.3 = f32[32,4,128]{2,1,0:T(4,128)S(1)} async-done(((f32[32,4,128]{2,1,0:T(4,128)}), f32[32,4,128]{2,1,0:T(4,128)S(1)}, u32[]{:S(2)}, u32[]{:S(2)}) %all-to-all-start.3) | async-done | bytes 65568 | tf_op jit(solution)/shard_map/all_to_all | solution.py:296
  40.6 0.7 %shard_map.79 = (f32[8,128]{1,0:T(8,128)}, f32[8,128]{1,0:T(8,128)}, s32[1]{0:T(128)}, s32[1]{0:T(128)}) custom-call(s32[1]{0:T(128)} %bitcast.3.row_ref, s32[1]{0:T(128)} %bitcast.4.col_ref, s32[1]{0:T(128)} %constant.29.clone.1.base_ref, f32[128,128]{1,0:T(8,128)S(1)} %bitcast.16), custom_call_target="tpu_custom_call" | custom-call | flops 1000000 | bytes 1000000 | tf_op jit(solution)/shard_map/pallas_call | solution.py:284
  41.4 0.6 %while.19 = (s32[1]{0:T(128)}, s32[1]{0:T(128)}, f32[512,128]{1,0:T(8,128)S(1)}, f32[512,128]{1,0:T(8,128)}, f32[1,2048]{1,0:T(1,128)}, /*index=5*/f32[8,128]{1,...) while((s32[1]{0:T(128)}, s32[1]{0:T(128)}, ...), condition=%region_1.0_spmd, body=%region_0.0_spmd | while | flops 4003000064 | bytes 5114329 | solution.py:359
  42.0 0.0 copy-start.2
  42.0 0.0 copy-start.7
  42.0 3.4 %all-to-all-start.4 = ((f32[8,1,128]{2,1,0:T(1,128)}), f32[8,1,128]{2,1,0:T(1,128)S(1)}, u32[]{:S(2)}, u32[]{:S(2)}) async-start(f32[8,1,128]{2,1,0:T(1,128)} %bitcast.24), calls=%async_computation.4 | async-start | bytes 8192 | tf_op jit(solution)/shard_map/all_to_all | solution.py:296
  45.5 0.0 copy-done.7
  45.5 1.7 %shard_map.81 = f32[512,128]{1,0:T(8,128)} custom-call(f32[512,128]{1,0:T(8,128)} %get-tuple-element.121.within_ref, f32[8,128]{1,0:T(8,128)S(1)} %copy-done.7), custom_call_target="tpu_custom_call" | custom-call | flops 4000000000 | bytes 1000000 | tf_op jit(solution)/shard_map/pallas_call | solution.py:284
  47.2 0.0 copy-done.2
  47.2 0.0 copy-start.6
  47.2 4.8 %all-to-all-done.4 = f32[8,1,128]{2,1,0:T(1,128)S(1)} async-done(((f32[8,1,128]{2,1,0:T(1,128)}), f32[8,1,128]{2,1,0:T(1,128)S(1)}, u32[]{:S(2)}, u32[]{:S(2)}) %all-to-all-start.4) | async-done | bytes 4128 | tf_op jit(solution)/shard_map/all_to_all | solution.py:296
  51.9 0.0 copy-done.6
  51.9 0.7 %shard_map.82 = f32[16,128]{1,0:T(8,128)} custom-call(f32[8,128]{1,0:T(8,128)S(1)} %copy-done.7, f32[8,128]{1,0:T(8,128)S(1)} %bitcast.17, s32[16,128]{1,0:T(8,128)S(1)} %bitcast.21, f32[16,128]{1,0:T(8,128)S(1)} %bitcast.18, f32[16,128]{1,0:T(8,128)S(1)} %bitcast.22), custom_call_target="tpu_custom_call" | custom-call | flops 1000000 | bytes 1000000 | tf_op jit(solution)/shard_map/pallas_call | solution.py:284
Async XLA Ops:
  0.6 0.8 %copy-start.3 = (s32[4,2048]{1,0:T(4,128)S(1)}, s32[4,2048]{1,0:T(4,128)}, u32[]{:S(2)}) copy-start(s32[4,2048]{1,0:T(4,128)} %boxes_ref.1) | copy-start | bytes 98308
  0.6 0.7 %copy-start.4 = (s32[2048]{0:T(1024)S(1)}, s32[2048]{0:T(1024)}, u32[]{:S(2)}) copy-start(s32[2048]{0:T(1024)} %param.8) | copy-start | bytes 24580
  3.4 11.3 %copy-start = (f32[1,2048]{1,0:T(1,128)S(1)}, f32[1,2048]{1,0:T(1,128)}, u32[]{:S(2)}) copy-start(f32[1,2048]{1,0:T(1,128)} %area_ref.1) | copy-start | bytes 24580
  3.4 11.3 %copy-start.5 = (s32[1,2048]{1,0:T(1,128)S(1)}, s32[1,2048]{1,0:T(1,128)}, u32[]{:S(2)}) copy-start(s32[1,2048]{1,0:T(1,128)} %bins_ref.3) | copy-start | bytes 24580
  3.4 20.5 %all-to-all-start.2 = ((f32[32,8,128]{2,1,0:T(8,128)}), f32[32,8,128]{2,1,0:T(8,128)S(1)}, u32[]{:S(2)}, u32[]{:S(2)}) async-start(f32[32,8,128]{2,1,0:T(8,128)} %shard_map.76), calls=%async_computation.2 | async-start | bytes 262144 | tf_op jit(solution)/shard_map/all_to_all | solution.py:296
  14.7 9.2 %copy-start.1 = (f32[512,128]{1,0:T(8,128)S(1)}, f32[512,128]{1,0:T(8,128)}, u32[]{:S(2)}) copy-start(f32[512,128]{1,0:T(8,128)} %capacity_ref.1) | copy-start | bytes 786436
  25.9 14.7 %all-to-all-start.3 = ((f32[32,4,128]{2,1,0:T(4,128)}), f32[32,4,128]{2,1,0:T(4,128)S(1)}, u32[]{:S(2)}, u32[]{:S(2)}) async-start(f32[32,4,128]{2,1,0:T(4,128)} %bitcast.7), calls=%async_computation.3 | async-start | bytes 131072 | tf_op jit(solution)/shard_map/all_to_all | solution.py:296
  42.0 5.2 %copy-start.2 = (f32[512,128]{1,0:T(8,128)}, f32[512,128]{1,0:T(8,128)S(1)}, u32[]{:S(2)}) copy-start(f32[512,128]{1,0:T(8,128)S(1)} %get-tuple-element.106) | copy-start | bytes 786436
  42.0 3.4 %copy-start.7 = (f32[8,128]{1,0:T(8,128)S(1)}, f32[8,128]{1,0:T(8,128)}, u32[]{:S(2)}) copy-start(f32[8,128]{1,0:T(8,128)} %get-tuple-element.122.carried_ref) | copy-start | bytes 12292
  42.0 9.9 %all-to-all-start.4 = ((f32[8,1,128]{2,1,0:T(1,128)}), f32[8,1,128]{2,1,0:T(1,128)S(1)}, u32[]{:S(2)}, u32[]{:S(2)}) async-start(f32[8,1,128]{2,1,0:T(1,128)} %bitcast.24), calls=%async_computation.4 | async-start | bytes 8192 | tf_op jit(solution)/shard_map/all_to_all | solution.py:296
  47.2 4.8 %copy-start.6 = (f32[1,2048]{1,0:T(1,128)S(1)}, f32[1,2048]{1,0:T(1,128)}, u32[]{:S(2)}) copy-start(f32[1,2048]{1,0:T(1,128)} %get-tuple-element.124) | copy-start | bytes 24580

commit v5 on v4

--- a/solution.py
+++ b/solution.py
@@ -36,11 +36,12 @@
 
 
 def pack_kernel(
-    peers, groups, group_cols, tile_rows, row_ref, base_ref, boxes_ref, pins_ref, out_ref, vals_ref
+    peers, groups, group_cols, tile_rows, boxes_ref, pins_ref, *refs
 ):
     nets = boxes_ref.shape[1]
-    row_start = row_ref[0]
-    base = base_ref[0]
+    *base_ref, out_ref, vals_ref = refs
+    base = base_ref[0][0] if base_ref else jnp.int32(0)
+    row_start = lax.axis_index(ROW) * tile_rows
     first_x, last_x = boxes_ref[0:1, :], boxes_ref[1:2, :]
     first_y, last_y = boxes_ref[2:3, :], boxes_ref[3:4, :]
     span_x = (last_x - first_x + 1).astype(F32)
@@ -137,8 +138,6 @@
 
 def tile_kernel(
     has_past,
-    row_ref,
-    col_ref,
     nets_ref,
     capacity_ref,
     below_ref,
@@ -147,10 +146,10 @@
 ):
     if has_past:
         past_ref, *refs = refs
-    rudy_ref, excess_ref, pay_ref = refs
+    rudy_ref, pay_ref = refs
     tile_rows, tile_cols = capacity_ref.shape
-    row_start = row_ref[0]
-    col_start = col_ref[0]
+    row_start = lax.axis_index(ROW) * tile_rows
+    col_start = lax.axis_index(COL) * tile_cols
     peers = nets_ref.shape[0]
     half = 256
     at = iota((half, SLOTS), 0).astype(F32).astype(BF16)
@@ -182,7 +181,6 @@
         rudy = rudy + past_ref[...]
     rudy_ref[...] = rudy
     excess = jnp.maximum(rudy - capacity_ref[...], 0.0)
-    excess_ref[...] = excess
     col_sum = jnp.sum(excess, axis=0, keepdims=True)
     weighed = jnp.sum(excess * below_ref[...], axis=0, keepdims=True)
     at = iota((8, LANES), 0) & 3
@@ -200,14 +198,17 @@
     return jnp.where(lower, a + pltpu.roll(a, half, 1), b + pltpu.roll(b, half, 1))
 
 
-def lookup_kernel(excess_ref, bins_ref, within_ref, looked_ref):
-    tile_rows, tile_cols = excess_ref.shape
+def inflation_kernel(
+    factor, rudy_ref, capacity_ref, bins_ref, carried_ref, inflation_ref, looked_ref
+):
+    tile_rows, tile_cols = rudy_ref.shape
+    excess = jnp.maximum(rudy_ref[...] - capacity_ref[...], 0.0)
     half = 256
     lower = (iota((half, half), 0) >= iota((half, half), 1)).astype(F32).astype(BF16)
     carry = jnp.zeros((1, tile_cols), F32)
     parts = []
     for start in range(0, tile_rows, half):
-        pieces = jnp.concatenate(three_parts(excess_ref[start : start + half]), axis=1)
+        pieces = jnp.concatenate(three_parts(excess[start : start + half]), axis=1)
         sums = contract(lower, pieces, 1, 0)
         part = (
             sums[:, :tile_cols]
@@ -218,7 +219,7 @@
         parts.append(part)
         carry = part[half - 1 : half, :]
     within = jnp.concatenate(parts, axis=0)
-    within_ref[...] = within
+    inflation_ref[...] = 1.0 + factor * (within + carried_ref[0:1])
 
     cells = bins_ref.shape[1]
     bin_row = lax.shift_right_logical(bins_ref[...], 7)
@@ -233,10 +234,11 @@
     looked_ref[...] = jnp.sum(jnp.where(is_col, picked, 0.0), axis=0, keepdims=True)
 
 
-def carry_kernel(
-    rows, factor, row_ref, col_ref, base_ref, pays_ref, carried_ref, totals_ref, base_out, left_ref
-):
-    row_me, col_me = row_ref[0], col_ref[0]
+def carry_kernel(rows, pays_ref, *refs):
+    *base_ref, carried_ref, totals_ref, base_out, left_ref = refs
+    base = (base_ref[0][0] if base_ref else 0) + SLOTS
+    row_me = lax.axis_index(ROW)
+    col_me = lax.axis_index(("col_1", "col_2"))
     width = pays_ref.shape[0] // (4 * rows)
     mine = jnp.zeros((1, LANES), F32)
     bilinear = jnp.zeros((1, LANES), F32)
@@ -252,15 +254,11 @@
             shared = shared + pay[2:3]
             largest = jnp.maximum(largest, pay[3:4])
             running = running + pay[0:1]
-    base_out[0] = base_ref[0] + SLOTS
-    left_ref[0] = jnp.max(largest).astype(jnp.int32) - (base_ref[0] + SLOTS)
+    base_out[0] = jnp.int32(base)
+    left_ref[0] = jnp.max(largest).astype(jnp.int32) - base
     carried_ref[...] = jnp.broadcast_to(mine, carried_ref.shape)
     totals = shared + halves(jnp.zeros((1, LANES), F32), bilinear)
     totals_ref[...] = jnp.broadcast_to(totals, totals_ref.shape)
-
-
-def inflation_kernel(factor, within_ref, carried_ref, inflation_ref):
-    inflation_ref[...] = 1.0 + factor * (within_ref[...] + carried_ref[0:1])
 
 
 def sizes_kernel(factor, carried_ref, totals_ref, bins_ref, area_ref, looked_ref, sizes_ref):
@@ -303,11 +301,7 @@
     nets = boxes.shape[1]
     cells = cell_bin.shape[1]
     factor = 2.0 / (tile_rows * rows)
-    row_at = lax.axis_index(ROW)[None]
     near = lax.axis_size(NEAR)
-    near_at = lax.axis_index(("col_1", "col_2"))[None]
-    row_start = row_at * tile_rows
-    col_start = lax.axis_index(COL)[None] * tile_cols
     pins = pins.reshape(1, nets)
     below, cell_sums = call(
         functools.partial(cells_kernel, tile_rows, tile_cols),
@@ -322,48 +316,47 @@
                 pack_kernel, cols, groups, tile_cols * (cols // groups), tile_rows
             ),
             [(cols, 8, SLOTS)],
-            (row_start, base, boxes, pins),
+            (boxes, pins) + base,
             [pltpu.VMEM((16, nets), F32)],
         )
         mine = exchange(packed, COL)
-        rudy, excess, pay = call(
+        rudy, pay = call(
             functools.partial(tile_kernel, past is not None),
-            [(tile_rows, tile_cols), (tile_rows, tile_cols), (near * 4, LANES)],
-            (row_start, col_start, mine, capacity, below, cell_sums)
+            [(tile_rows, tile_cols), (near * 4, LANES)],
+            (mine, capacity, below, cell_sums)
             + (() if past is None else (past,)),
             limit=28,
         )
         pays = exchange(pay.reshape(near, 4, LANES), NEAR).reshape(near * 4, LANES)
-        within, looked = call(
-            lookup_kernel,
-            [(tile_rows, tile_cols), (1, cells)],
-            (excess, cell_bin),
-            limit=28,
-            flops=4_000_000_000,
-        )
         one = jax.ShapeDtypeStruct((1,), jnp.int32)
-        carried, totals, base, left = call(
-            functools.partial(carry_kernel, rows, factor),
+        carried, totals, reached, left = call(
+            functools.partial(carry_kernel, rows),
             [(8, LANES), (groups, LANES), one, one],
-            (row_at, near_at, base, pays),
-        )
-        return left, base, rudy, within, looked, carried, totals
+            (pays,) + base,
+        )
+        return left, reached, rudy, carried, totals
 
     def unfinished(state):
         return state[0][0] > 0
 
     def next_round(state):
-        return one_round(state[1], state[2])
-
-    first = one_round(jnp.zeros((1,), jnp.int32), None)
-    _, _, rudy, within, looked, carried, totals = lax.while_loop(unfinished, next_round, first)
+        return one_round((state[1],), state[2])
+
+    first = one_round((), None)
+    _, _, rudy, carried, totals = lax.cond(
+        unfinished(first),
+        lambda state: lax.while_loop(unfinished, next_round, state),
+        lambda state: state,
+        first,
+    )
 
     totals = exchange(totals, "col_0")
     shape = (cells // LANES, LANES)
-    (inflation,) = call(
+    inflation, looked = call(
         functools.partial(inflation_kernel, factor),
-        [(tile_rows, tile_cols)],
-        (within, carried),
+        [(tile_rows, tile_cols), (1, cells)],
+        (rudy, capacity, cell_bin, carried),
+        limit=28,
         flops=4_000_000_000,
     )
     (sizes,) = call(

time: 53.1 us -> 52.3 us (0.985)
  blocking collectives: 0 us -> 14.5 us
  starting transfers between devices: 22 us -> 14.7 us
  waiting for transfers between devices: 18.1 us -> 12.6 us
  Pallas kernels: 10.4 us -> 8.66 us
  local copies, waits for them, and re-layouts: 0.76 us -> 0.07 us
  loops' own time: 0.64 us -> 0.01 us
  between operations: 0.76 us -> 1.35 us
    all_to_all x0 -> x1, blocking collectives: none -> 14.5 us  [exchange(): return lax.all_to_all(payload, axis, 0, 0, tiled=True)]
    all_to_all x3 -> x2, starting transfers between devices: 22 us -> 14.7 us  [exchange(): return lax.all_to_all(payload, axis, 0, 0, tiled=True)]
    all_to_all x3 -> x2, waiting for transfers between devices: 18.1 us -> 12.6 us  [exchange(): return lax.all_to_all(payload, axis, 0, 0, tiled=True)]
    pallas_call x7 -> x6, Pallas kernels: 10.4 us -> 8.66 us  [call(): pl.pallas_call(kernel, out_shape=outs, in_specs=[smem if a.ndim == 1 else...]
    unnamed x16 -> x14, local copies, waits for them, and re-layouts: 0.76 us -> 0.07 us
    another operation x1, loops' own time: 0.64 us -> 0.01 us  [per_device(): lax.cond(unfinished(first), lambda state: lax.while_loop(unfinished, next...]
  transfers between devices with their start and end apart: 3 -> 2, of which waited for: 3 -> 2; matrix products, arithmetic and copies ran while one was open for 0% -> 0% of each run, Pallas kernels for 9% -> 6%
where the time goes in v5:
time: 52.3 us; the launch traced here: 51.9 us
  starting transfers between devices  14.7 us (28%)
  blocking collectives  14.5 us (28%)
  waiting for transfers between devices  12.6 us (24%)
  Pallas kernels  8.66 us (17%)
  between operations  1.35 us (3%)
    all_to_all x2, starting transfers between devices, exchange(): return lax.all_to_all(payload, axis, 0, 0, tiled=True)  14.7 us
    all_to_all x1, blocking collectives, exchange(): return lax.all_to_all(payload, axis, 0, 0, tiled=True)  14.5 us
    all_to_all x2, waiting for transfers between devices, exchange(): return lax.all_to_all(payload, axis, 0, 0, tiled=True)  12.6 us
    pallas_call x6, Pallas kernels, call(): pl.pallas_call(kernel, out_shape=outs, in_specs=[smem if a.ndim == 1 else...  8.66 us
  transfers between devices with their start and end apart: 2, of which 2 were waited for; matrix products, arithmetic and copies ran while one was open for 0% of the time, Pallas kernels for 6%

profile of v5, /device:TPU:1, one launch (start us, length us, event | category | flops | bytes accessed | tf_op | source)
XLA Modules:
  0.0 51.9 jit_solution(4308403644511147740)
XLA Ops:
  0.6 2.8 %shard_map.76 = f32[32,8,128]{2,1,0:T(8,128)} custom-call(s32[4,2048]{1,0:T(4,128)} %boxes_ref.1, s32[1,2048]{1,0:T(1,128)} %bitcast.21), custom_call_target="tpu_custom_call" | custom-call | flops 1000000 | bytes 1000000 | tf_op jit(solution)/shard_map/pallas_call | solution.py:282
  3.4 0.0 copy-start
  3.4 0.0 copy-start.1
  3.4 11.3 %all-to-all-start.2 = ((f32[32,8,128]{2,1,0:T(8,128)}), f32[32,8,128]{2,1,0:T(8,128)S(1)}, u32[]{:S(2)}, u32[]{:S(2)}) async-start(f32[32,8,128]{2,1,0:T(8,128)} %shard_map.76), calls=%async_computation.2 | async-start | bytes 262144 | tf_op jit(solution)/shard_map/all_to_all | solution.py:294
  14.7 0.0 copy-done
  14.7 0.0 copy-done.1
  14.7 0.0 copy-start.2
  14.7 1.3 %shard_map.77 = (f32[512,128]{1,0:T(8,128)S(1)}, f32[8,128]{1,0:T(8,128)S(1)}) custom-call(s32[1,2048]{1,0:T(1,128)S(1)} %copy-done, f32[1,2048]{1,0:T(1,128)S(1)} %copy-done.1), custom_call_target="tpu_custom_call" | custom-call | flops 4000000000 | bytes 1000000 | tf_op jit(solution)/shard_map/pallas_call | solution.py:282
  16.0 7.9 %all-to-all-done.2.nets_ref = f32[32,8,128]{2,1,0:T(8,128)S(1)} async-done(((f32[32,8,128]{2,1,0:T(8,128)}), f32[32,8,128]{2,1,0:T(8,128)S(1)}, u32[]{:S(2)}, u32[]{:S(2)}) %all-to-all-start.2) | async-done | bytes 131104 | tf_op jit(solution)/shard_map/all_to_all | solution.py:294
  23.9 0.0 copy-done.2
  23.9 1.4 %shard_map.78 = (f32[512,128]{1,0:T(8,128)S(1)}, f32[128,128]{1,0:T(8,128)S(1)}) custom-call(f32[32,8,128]{2,1,0:T(8,128)S(1)} %all-to-all-done.2.nets_ref, f32[512,128]{1,0:T(8,128)S(1)} %copy-done.2, f32[512,128]{1,0:T(8,128)S(1)} %get-tuple-element.109.below_ref, f32[8,128]{1,0:T(8,128)S(1)} %get-tuple-element.110.sums_ref), custom_call_target="tpu_custom_call" | custom-call | flops 1000000 | bytes 1000000 | tf_op jit(solution)/shard_map/pallas_call | solution.py:282
  25.3 14.5 %all_to_all.30 = f32[32,4,128]{2,1,0:T(4,128)S(1)} all-to-all(f32[32,4,128]{2,1,0:T(4,128)S(1)} %bitcast.16), channel_id=1, replica_groups=mesh['row_0'=4,'row_1'=2,'col_0'=8,'col_1'=2,'col_2'=2] {'row_0','row_1'..., dimensions={0} | all-to-all | bytes 131072 | tf_op jit(solution)/shard_map/all_to_all | solution.py:294
  39.8 0.0 copy-start.4
  39.8 0.7 %shard_map.79 = (f32[8,128]{1,0:T(8,128)}, f32[8,128]{1,0:T(8,128)}, s32[1]{0:T(128)}, s32[1]{0:T(128)}) custom-call(f32[128,128]{1,0:T(8,128)S(1)} %bitcast.15), custom_call_target="tpu_custom_call" | custom-call | flops 1000000 | bytes 1000000 | tf_op jit(solution)/shard_map/pallas_call | solution.py:282
  40.5 0.0 copy-start.5
  41.2 0.0 copy-done.4
  41.2 0.0 copy-done.5
  41.2 0.0 copy-start.3
  41.2 0.0 copy-start.6
  41.2 3.4 %all-to-all-start.4 = ((f32[8,1,128]{2,1,0:T(1,128)}), f32[8,1,128]{2,1,0:T(1,128)S(1)}, u32[]{:S(2)}, u32[]{:S(2)}) async-start(f32[8,1,128]{2,1,0:T(1,128)} %bitcast.7), calls=%async_computation.4 | async-start | bytes 8192 | tf_op jit(solution)/shard_map/all_to_all | solution.py:294
  44.7 0.0 copy-done.6
  44.7 1.8 %shard_map.80 = (f32[512,128]{1,0:T(8,128)}, f32[1,2048]{1,0:T(1,128)S(1)}) custom-call(f32[512,128]{1,0:T(8,128)S(1)} %get-tuple-element.106.rudy_ref, f32[512,128]{1,0:T(8,128)S(1)} %copy-done.2, s32[1,2048]{1,0:T(1,128)S(1)} %copy-done, f32[8,128]{1,0:T(8,128)S(1)} %copy-done.6), custom_call_target="tpu_custom_call" | custom-call | flops 4000000000 | bytes 1000000 | tf_op jit(solution)/shard_map/pallas_call | solution.py:282
  46.5 0.0 copy-done.3
  46.5 4.7 %all-to-all-done.4 = f32[8,1,128]{2,1,0:T(1,128)S(1)} async-done(((f32[8,1,128]{2,1,0:T(1,128)}), f32[8,1,128]{2,1,0:T(1,128)S(1)}, u32[]{:S(2)}, u32[]{:S(2)}) %all-to-all-start.4) | async-done | bytes 4128 | tf_op jit(solution)/shard_map/all_to_all | solution.py:294
  51.2 0.7 %shard_map.81 = f32[16,128]{1,0:T(8,128)} custom-call(f32[8,128]{1,0:T(8,128)S(1)} %copy-done.6, f32[8,128]{1,0:T(8,128)S(1)} %bitcast.17, s32[16,128]{1,0:T(8,128)S(1)} %bitcast.18, f32[16,128]{1,0:T(8,128)S(1)} %bitcast.19, f32[16,128]{1,0:T(8,128)S(1)} %bitcast.20), custom_call_target="tpu_custom_call" | custom-call | flops 1000000 | bytes 1000000 | tf_op jit(solution)/shard_map/pallas_call | solution.py:282
  (1 shorter events, 0.0 us)
Async XLA Ops:
  3.4 11.3 %copy-start = (s32[1,2048]{1,0:T(1,128)S(1)}, s32[1,2048]{1,0:T(1,128)}, u32[]{:S(2)}) copy-start(s32[1,2048]{1,0:T(1,128)} %bins_ref.3) | copy-start | bytes 24580
  3.4 11.3 %copy-start.1 = (f32[1,2048]{1,0:T(1,128)S(1)}, f32[1,2048]{1,0:T(1,128)}, u32[]{:S(2)}) copy-start(f32[1,2048]{1,0:T(1,128)} %area_ref.1) | copy-start | bytes 24580
  3.4 20.5 %all-to-all-start.2 = ((f32[32,8,128]{2,1,0:T(8,128)}), f32[32,8,128]{2,1,0:T(8,128)S(1)}, u32[]{:S(2)}, u32[]{:S(2)}) async-start(f32[32,8,128]{2,1,0:T(8,128)} %shard_map.76), calls=%async_computation.2 | async-start | bytes 262144 | tf_op jit(solution)/shard_map/all_to_all | solution.py:294
  14.7 9.2 %copy-start.2 = (f32[512,128]{1,0:T(8,128)S(1)}, f32[512,128]{1,0:T(8,128)}, u32[]{:S(2)}) copy-start(f32[512,128]{1,0:T(8,128)} %capacity_ref.3) | copy-start | bytes 786436
  39.8 1.4 %copy-start.4 = (s32[4,2048]{1,0:T(4,128)S(1)}, s32[4,2048]{1,0:T(4,128)}, u32[]{:S(2)}) copy-start(s32[4,2048]{1,0:T(4,128)} %boxes_ref.1) | copy-start | bytes 98308
  40.5 0.7 %copy-start.5 = (s32[2048]{0:T(1024)S(1)}, s32[2048]{0:T(1024)}, u32[]{:S(2)}) copy-start(s32[2048]{0:T(1024)} %param.10) | copy-start | bytes 24580
  41.2 5.2 %copy-start.3 = (f32[512,128]{1,0:T(8,128)}, f32[512,128]{1,0:T(8,128)S(1)}, u32[]{:S(2)}) copy-start(f32[512,128]{1,0:T(8,128)S(1)} %get-tuple-element.106.rudy_ref) | copy-start | bytes 786436
  41.2 3.4 %copy-start.6 = (f32[8,128]{1,0:T(8,128)S(1)}, f32[8,128]{1,0:T(8,128)}, u32[]{:S(2)}) copy-start(f32[8,128]{1,0:T(8,128)} %get-tuple-element.118.carried_ref) | copy-start | bytes 12292
  41.2 9.9 %all-to-all-start.4 = ((f32[8,1,128]{2,1,0:T(1,128)}), f32[8,1,128]{2,1,0:T(1,128)S(1)}, u32[]{:S(2)}, u32[]{:S(2)}) async-start(f32[8,1,128]{2,1,0:T(1,128)} %bitcast.7), calls=%async_computation.4 | async-start | bytes 8192 | tf_op jit(solution)/shard_map/all_to_all | solution.py:294

commit v6 on v5

--- a/solution.py
+++ b/solution.py
@@ -1,4 +1,5 @@
 import functools
+import math
 
 import jax
 import jax.numpy as jnp
@@ -36,7 +37,7 @@
 
 
 def pack_kernel(
-    peers, groups, group_cols, tile_rows, boxes_ref, pins_ref, *refs
+    order, peers, groups, group_cols, tile_rows, boxes_ref, pins_ref, *refs
 ):
     nets = boxes_ref.shape[1]
     *base_ref, out_ref, vals_ref = refs
@@ -89,8 +90,9 @@
         got = contract(vals, chosen, 1, 1)
         row = got[0:8] * 256.0 + got[8:16]
         row = jnp.where(field == 5, jnp.broadcast_to(largest, (8, SLOTS)), row)
-        for peer in range(group * (peers // groups), (group + 1) * (peers // groups)):
-            out_ref[peer] = row
+        for at, peer in enumerate(order):
+            if peer * groups // peers == group:
+                out_ref[at] = row
 
 
 def cells_kernel(tile_rows, tile_cols, bins_ref, area_ref, below_ref, sums_ref):
@@ -234,7 +236,7 @@
     looked_ref[...] = jnp.sum(jnp.where(is_col, picked, 0.0), axis=0, keepdims=True)
 
 
-def carry_kernel(rows, pays_ref, *refs):
+def carry_kernel(order, rows, pays_ref, *refs):
     *base_ref, carried_ref, totals_ref, base_out, left_ref = refs
     base = (base_ref[0][0] if base_ref else 0) + SLOTS
     row_me = lax.axis_index(ROW)
@@ -247,7 +249,7 @@
     for col in range(width):
         running = jnp.zeros((1, LANES), F32)
         for row in range(rows):
-            at = 4 * (row * width + col)
+            at = 4 * order.index(row * width + col)
             pay = pays_ref[at : at + 4]
             mine = jnp.where((row_me == row) & (col_me == col), running, mine)
             bilinear = bilinear + pay[1:2] * running
@@ -290,8 +292,37 @@
     )(*args)
 
 
-def exchange(payload, axis):
-    return lax.all_to_all(payload, axis, 0, 0, tiled=True)
+def hops(a, b, size):
+    return min((a - b) % size, (b - a) % size)
+
+
+def peer_order(names):
+    sizes = [lax.axis_size(name) for name in names]
+    full = {name: lax.axis_size(name) for name in ROW + COL}
+    y_size = full["row_1"] * full["col_1"]
+    places = []
+    for index in range(math.prod(sizes)):
+        at, rest = {}, index
+        for name, size in reversed(list(zip(names, sizes))):
+            at[name] = rest % size
+            rest //= size
+        away = 0.0
+        for name in ("row_0", "col_0"):
+            if name in at:
+                away += hops(at[name], full[name] // 2, full[name])
+        if "row_1" in at:
+            away += hops(at["row_1"] * full["col_1"] + at["col_1"], y_size // 2, y_size)
+        elif "col_1" in at:
+            away += full["col_1"] - 1 - at["col_1"]
+        if "col_2" in at:
+            away += 0.5 * (full["col_2"] - 1 - at["col_2"])
+        places.append((-away, index))
+    root = max(places)
+    return [root[1]] + [p[1] for p in sorted(places) if p != root]
+
+
+def exchange(payload, axis, order):
+    return lax.all_to_all(payload, axis, 0, 0, axis_index_groups=[order], tiled=True)
 
 
 def per_device(boxes, pins, capacity, cell_bin, cell_area):
@@ -302,6 +333,9 @@
     cells = cell_bin.shape[1]
     factor = 2.0 / (tile_rows * rows)
     near = lax.axis_size(NEAR)
+    col_order = peer_order(COL)
+    near_order = peer_order(NEAR)
+    far_order = peer_order(("col_0",))
     pins = pins.reshape(1, nets)
     below, cell_sums = call(
         functools.partial(cells_kernel, tile_rows, tile_cols),
@@ -313,13 +347,13 @@
     def one_round(base, past):
         (packed,) = call(
             functools.partial(
-                pack_kernel, cols, groups, tile_cols * (cols // groups), tile_rows
+                pack_kernel, col_order, cols, groups, tile_cols * (cols // groups), tile_rows
             ),
             [(cols, 8, SLOTS)],
             (boxes, pins) + base,
             [pltpu.VMEM((16, nets), F32)],
         )
-        mine = exchange(packed, COL)
+        mine = exchange(packed, COL, col_order)
         rudy, pay = call(
             functools.partial(tile_kernel, past is not None),
             [(tile_rows, tile_cols), (near * 4, LANES)],
@@ -327,10 +361,10 @@
             + (() if past is None else (past,)),
             limit=28,
         )
-        pays = exchange(pay.reshape(near, 4, LANES), NEAR).reshape(near * 4, LANES)
+        pays = exchange(pay.reshape(near, 4, LANES), NEAR, near_order).reshape(near * 4, LANES)
         one = jax.ShapeDtypeStruct((1,), jnp.int32)
         carried, totals, reached, left = call(
-            functools.partial(carry_kernel, rows),
+            functools.partial(carry_kernel, near_order, rows),
             [(8, LANES), (groups, LANES), one, one],
             (pays,) + base,
         )
@@ -350,7 +384,7 @@
         first,
     )
 
-    totals = exchange(totals, "col_0")
+    totals = exchange(totals, "col_0", far_order)
     shape = (cells // LANES, LANES)
     inflation, looked = call(
         functools.partial(inflation_kernel, factor),

time: 52.3 us -> 44.7 us (0.85)
  waiting for transfers between devices: 12.6 us -> 3.02 us
  starting transfers between devices: 14.7 us -> 20.2 us
  blocking collectives: 14.5 us -> 11 us
    all_to_all x2, waiting for transfers between devices: 12.6 us -> 3.02 us  [exchange(): lax.all_to_all(payload, axis, 0, 0, axis_index_groups=[order], tiled=True)]
    all_to_all x2, starting transfers between devices: 14.7 us -> 20.2 us  [exchange(): lax.all_to_all(payload, axis, 0, 0, axis_index_groups=[order], tiled=True)]
    all_to_all x1, blocking collectives: 14.5 us -> 11 us  [exchange(): lax.all_to_all(payload, axis, 0, 0, axis_index_groups=[order], tiled=True)]
  transfers between devices with their start and end apart: 2 -> 2, of which waited for: 2 -> 1; matrix products, arithmetic and copies ran while one was open for 0% -> 0% of each run, Pallas kernels for 6% -> 7%
where the time goes in v6:
time: 44.7 us; the launch traced here: 44.3 us
  starting transfers between devices  20.2 us (45%)
  blocking collectives  11 us (25%)
  Pallas kernels  8.66 us (19%)
  waiting for transfers between devices  3.02 us (7%)
  between operations  1.34 us (3%)
    all_to_all x2, starting transfers between devices, exchange(): lax.all_to_all(payload, axis, 0, 0, axis_index_groups=[order], tiled=True)  20.2 us
    all_to_all x1, blocking collectives, exchange(): lax.all_to_all(payload, axis, 0, 0, axis_index_groups=[order], tiled=True)  11 us
    pallas_call x6, Pallas kernels, call(): pl.pallas_call(kernel, out_shape=outs, in_specs=[smem if a.ndim == 1 else...  8.66 us
    all_to_all x2, waiting for transfers between devices, exchange(): lax.all_to_all(payload, axis, 0, 0, axis_index_groups=[order], tiled=True)  3.02 us
  transfers between devices with their start and end apart: 2, of which 1 were waited for; matrix products, arithmetic and copies ran while one was open for 0% of the time, Pallas kernels for 7%

profile of v6, /device:TPU:1, one launch (start us, length us, event | category | flops | bytes accessed | tf_op | source)
XLA Modules:
  0.0 44.3 jit_solution(6528358026173083559)
XLA Ops:
  0.6 2.8 %shard_map.76 = f32[32,8,128]{2,1,0:T(8,128)} custom-call(s32[4,2048]{1,0:T(4,128)} %boxes_ref.1, s32[1,2048]{1,0:T(1,128)} %bitcast.21), custom_call_target="tpu_custom_call" | custom-call | flops 1000000 | bytes 1000000 | tf_op jit(solution)/shard_map/pallas_call | solution.py:284
  3.4 0.0 copy-start
  3.4 0.0 copy-start.1
  3.4 12.5 %all-to-all-start.2 = ((f32[32,8,128]{2,1,0:T(8,128)}), f32[32,8,128]{2,1,0:T(8,128)S(1)}, u32[]{:S(2)}, u32[]{:S(2)}) async-start(f32[32,8,128]{2,1,0:T(8,128)} %shard_map.76), calls=%async_computation.2 | async-start | bytes 262144 | tf_op jit(solution)/shard_map/all_to_all | solution.py:325
  15.9 0.0 copy-done
  16.0 0.0 copy-done.1
  16.0 0.0 copy-start.2
  16.0 1.3 %shard_map.77 = (f32[512,128]{1,0:T(8,128)S(1)}, f32[8,128]{1,0:T(8,128)S(1)}) custom-call(s32[1,2048]{1,0:T(1,128)S(1)} %copy-done, f32[1,2048]{1,0:T(1,128)S(1)} %copy-done.1), custom_call_target="tpu_custom_call" | custom-call | flops 4000000000 | bytes 1000000 | tf_op jit(solution)/shard_map/pallas_call | solution.py:284
  17.3 3.0 %all-to-all-done.2.nets_ref = f32[32,8,128]{2,1,0:T(8,128)S(1)} async-done(((f32[32,8,128]{2,1,0:T(8,128)}), f32[32,8,128]{2,1,0:T(8,128)S(1)}, u32[]{:S(2)}, u32[]{:S(2)}) %all-to-all-start.2) | async-done | bytes 131104 | tf_op jit(solution)/shard_map/all_to_all | solution.py:325
  20.3 0.0 copy-done.2
  20.3 1.4 %shard_map.78 = (f32[512,128]{1,0:T(8,128)S(1)}, f32[128,128]{1,0:T(8,128)S(1)}) custom-call(f32[32,8,128]{2,1,0:T(8,128)S(1)} %all-to-all-done.2.nets_ref, f32[512,128]{1,0:T(8,128)S(1)} %copy-done.2, f32[512,128]{1,0:T(8,128)S(1)} %get-tuple-element.109.below_ref, f32[8,128]{1,0:T(8,128)S(1)} %get-tuple-element.110.sums_ref), custom_call_target="tpu_custom_call" | custom-call | flops 1000000 | bytes 1000000 | tf_op jit(solution)/shard_map/pallas_call | solution.py:284
  21.6 11.0 %all_to_all.30 = f32[32,4,128]{2,1,0:T(4,128)S(1)} all-to-all(f32[32,4,128]{2,1,0:T(4,128)S(1)} %bitcast.16), channel_id=1, replica_groups={{161,0,1,2,34,64,192,3,35,65,193,32,66,98,128,194,226,33,67,99,129,195,..., dimensions={0} | all-to-all | bytes 131072 | tf_op jit(solution)/shard_map/all_to_all | solution.py:325
  32.6 0.0 copy-start.4
  32.6 0.7 %shard_map.79 = (f32[8,128]{1,0:T(8,128)}, f32[8,128]{1,0:T(8,128)}, s32[1]{0:T(128)}, s32[1]{0:T(128)}) custom-call(f32[128,128]{1,0:T(8,128)S(1)} %bitcast.15), custom_call_target="tpu_custom_call" | custom-call | flops 1000000 | bytes 1000000 | tf_op jit(solution)/shard_map/pallas_call | solution.py:284
  33.4 0.0 copy-start.5
  34.0 0.0 copy-done.4
  34.0 0.0 copy-done.5
  34.1 0.0 copy-start.3
  34.1 0.0 copy-start.6
  34.1 7.7 %all-to-all-start.4 = ((f32[8,1,128]{2,1,0:T(1,128)}), f32[8,1,128]{2,1,0:T(1,128)S(1)}, u32[]{:S(2)}, u32[]{:S(2)}) async-start(f32[8,1,128]{2,1,0:T(1,128)} %bitcast.7), calls=%async_computation.4 | async-start | bytes 8192 | tf_op jit(solution)/shard_map/all_to_all | solution.py:325
  41.8 0.0 copy-done.6
  41.8 1.8 %shard_map.80 = (f32[512,128]{1,0:T(8,128)}, f32[1,2048]{1,0:T(1,128)S(1)}) custom-call(f32[512,128]{1,0:T(8,128)S(1)} %get-tuple-element.106.rudy_ref, f32[512,128]{1,0:T(8,128)S(1)} %copy-done.2, s32[1,2048]{1,0:T(1,128)S(1)} %copy-done, f32[8,128]{1,0:T(8,128)S(1)} %copy-done.6), custom_call_target="tpu_custom_call" | custom-call | flops 4000000000 | bytes 1000000 | tf_op jit(solution)/shard_map/pallas_call | solution.py:284
  43.6 0.0 copy-done.3
  43.6 0.0 all-to-all-done.4
  43.6 0.7 %shard_map.81 = f32[16,128]{1,0:T(8,128)} custom-call(f32[8,128]{1,0:T(8,128)S(1)} %copy-done.6, f32[8,128]{1,0:T(8,128)S(1)} %bitcast.17, s32[16,128]{1,0:T(8,128)S(1)} %bitcast.18, f32[16,128]{1,0:T(8,128)S(1)} %bitcast.19, f32[16,128]{1,0:T(8,128)S(1)} %bitcast.20), custom_call_target="tpu_custom_call" | custom-call | flops 1000000 | bytes 1000000 | tf_op jit(solution)/shard_map/pallas_call | solution.py:284
  (1 shorter events, 0.0 us)
Async XLA Ops:
  3.4 12.5 %copy-start = (s32[1,2048]{1,0:T(1,128)S(1)}, s32[1,2048]{1,0:T(1,128)}, u32[]{:S(2)}) copy-start(s32[1,2048]{1,0:T(1,128)} %bins_ref.3) | copy-start | bytes 24580
  3.4 12.5 %copy-start.1 = (f32[1,2048]{1,0:T(1,128)S(1)}, f32[1,2048]{1,0:T(1,128)}, u32[]{:S(2)}) copy-start(f32[1,2048]{1,0:T(1,128)} %area_ref.1) | copy-start | bytes 24580
  3.4 16.9 %all-to-all-start.2 = ((f32[32,8,128]{2,1,0:T(8,128)}), f32[32,8,128]{2,1,0:T(8,128)S(1)}, u32[]{:S(2)}, u32[]{:S(2)}) async-start(f32[32,8,128]{2,1,0:T(8,128)} %shard_map.76), calls=%async_computation.2 | async-start | bytes 262144 | tf_op jit(solution)/shard_map/all_to_all | solution.py:325
  16.0 4.3 %copy-start.2 = (f32[512,128]{1,0:T(8,128)S(1)}, f32[512,128]{1,0:T(8,128)}, u32[]{:S(2)}) copy-start(f32[512,128]{1,0:T(8,128)} %capacity_ref.3) | copy-start | bytes 786436
  32.6 1.4 %copy-start.4 = (s32[4,2048]{1,0:T(4,128)S(1)}, s32[4,2048]{1,0:T(4,128)}, u32[]{:S(2)}) copy-start(s32[4,2048]{1,0:T(4,128)} %boxes_ref.1) | copy-start | bytes 98308
  33.4 0.7 %copy-start.5 = (s32[2048]{0:T(1024)S(1)}, s32[2048]{0:T(1024)}, u32[]{:S(2)}) copy-start(s32[2048]{0:T(1024)} %param.10) | copy-start | bytes 24580
  34.1 9.5 %copy-start.3 = (f32[512,128]{1,0:T(8,128)}, f32[512,128]{1,0:T(8,128)S(1)}, u32[]{:S(2)}) copy-start(f32[512,128]{1,0:T(8,128)S(1)} %get-tuple-element.106.rudy_ref) | copy-start | bytes 786436
  34.1 7.7 %copy-start.6 = (f32[8,128]{1,0:T(8,128)S(1)}, f32[8,128]{1,0:T(8,128)}, u32[]{:S(2)}) copy-start(f32[8,128]{1,0:T(8,128)} %get-tuple-element.118.carried_ref) | copy-start | bytes 12292
  34.1 9.5 %all-to-all-start.4 = ((f32[8,1,128]{2,1,0:T(1,128)}), f32[8,1,128]{2,1,0:T(1,128)S(1)}, u32[]{:S(2)}, u32[]{:S(2)}) async-start(f32[8,1,128]{2,1,0:T(1,128)} %bitcast.7), calls=%async_computation.4 | async-start | bytes 8192 | tf_op jit(solution)/shard_map/all_to_all | solution.py:325

commit v7 on v6

--- a/solution.py
+++ b/solution.py
@@ -34,6 +34,11 @@
     middle = rest.astype(BF16)
     low = (rest - middle.astype(F32)).astype(BF16)
     return high, middle, low
+
+
+def two_parts(x):
+    high = x.astype(BF16)
+    return high, (x - high.astype(F32)).astype(BF16)
 
 
 def pack_kernel(
@@ -200,6 +205,10 @@
     return jnp.where(lower, a + pltpu.roll(a, half, 1), b + pltpu.roll(b, half, 1))
 
 
+def near_row(row, count):
+    return tall(jnp.clip(row.astype(F32), -1.0, float(count)), count)
+
+
 def inflation_kernel(
     factor, rudy_ref, capacity_ref, bins_ref, carried_ref, inflation_ref, looked_ref
 ):
@@ -210,14 +219,9 @@
     carry = jnp.zeros((1, tile_cols), F32)
     parts = []
     for start in range(0, tile_rows, half):
-        pieces = jnp.concatenate(three_parts(excess[start : start + half]), axis=1)
+        pieces = jnp.concatenate(two_parts(excess[start : start + half]), axis=1)
         sums = contract(lower, pieces, 1, 0)
-        part = (
-            sums[:, :tile_cols]
-            + sums[:, tile_cols : 2 * tile_cols]
-            + sums[:, 2 * tile_cols :]
-            + carry
-        )
+        part = sums[:, :tile_cols] + sums[:, tile_cols:] + carry
         parts.append(part)
         carry = part[half - 1 : half, :]
     within = jnp.concatenate(parts, axis=0)
@@ -226,12 +230,17 @@
     cells = bins_ref.shape[1]
     bin_row = lax.shift_right_logical(bins_ref[...], 7)
     bin_col = bins_ref[...] & 127
-    row_hot = jnp.where(iota((tile_rows, cells), 0) == bin_row, 1.0, 0.0).astype(BF16)
-    turned = jnp.concatenate(three_parts(within.T), axis=0)
+    at = iota((half, cells), 0).astype(F32).astype(BF16)
+    row_hot = jnp.concatenate(
+        [
+            jnp.where(at == near_row(bin_row - start, half), BF16(1), BF16(0))
+            for start in range(0, tile_rows, half)
+        ],
+        axis=0,
+    )
+    turned = jnp.concatenate(two_parts(within.T), axis=0)
     picked = contract(turned, row_hot, 1, 0)
-    picked = (
-        picked[:tile_cols] + picked[tile_cols : 2 * tile_cols] + picked[2 * tile_cols :]
-    )
+    picked = picked[:tile_cols] + picked[tile_cols:]
     is_col = iota((tile_cols, cells), 0) == bin_col
     looked_ref[...] = jnp.sum(jnp.where(is_col, picked, 0.0), axis=0, keepdims=True)
 
@@ -300,6 +309,7 @@
     sizes = [lax.axis_size(name) for name in names]
     full = {name: lax.axis_size(name) for name in ROW + COL}
     y_size = full["row_1"] * full["col_1"]
+    middle = full["col_0"] // 2 + (names == COL)
     places = []
     for index in range(math.prod(sizes)):
         at, rest = {}, index
@@ -307,13 +317,14 @@
             at[name] = rest % size
             rest //= size
         away = 0.0
-        for name in ("row_0", "col_0"):
-            if name in at:
-                away += hops(at[name], full[name] // 2, full[name])
+        if "row_0" in at:
+            away += hops(at["row_0"], full["row_0"] // 2, full["row_0"])
+        if "col_0" in at:
+            away += hops(at["col_0"], middle, full["col_0"])
         if "row_1" in at:
             away += hops(at["row_1"] * full["col_1"] + at["col_1"], y_size // 2, y_size)
         elif "col_1" in at:
-            away += full["col_1"] - 1 - at["col_1"]
+            away += at["col_1"]
         if "col_2" in at:
             away += 0.5 * (full["col_2"] - 1 - at["col_2"])
         places.append((-away, index))

time: 44.7 us -> 43.9 us (0.982)
  waiting for transfers between devices: 3.02 us -> 4.6 us
  starting transfers between devices: 20.2 us -> 18.8 us
  blocking collectives: 11 us -> 10.3 us
    all_to_all x2, waiting for transfers between devices: 3.02 us -> 4.6 us  [exchange(): lax.all_to_all(payload, axis, 0, 0, axis_index_groups=[order], tiled=True)]
    all_to_all x2, starting transfers between devices: 20.2 us -> 18.8 us  [exchange(): lax.all_to_all(payload, axis, 0, 0, axis_index_groups=[order], tiled=True)]
    all_to_all x1, blocking collectives: 11 us -> 10.3 us  [exchange(): lax.all_to_all(payload, axis, 0, 0, axis_index_groups=[order], tiled=True)]
  transfers between devices with their start and end apart: 2 -> 2, of which waited for: 1 -> 1; matrix products, arithmetic and copies ran while one was open for 0% -> 0% of each run, Pallas kernels for 7% -> 6%
where the time goes in v7:
time: 43.9 us; the launch traced here: 43.5 us
  starting transfers between devices  18.8 us (43%)
  blocking collectives  10.3 us (23%)
  Pallas kernels  8.35 us (19%)
  waiting for transfers between devices  4.6 us (10%)
  between operations  1.34 us (3%)
    all_to_all x2, starting transfers between devices, exchange(): lax.all_to_all(payload, axis, 0, 0, axis_index_groups=[order], tiled=True)  18.8 us
    all_to_all x1, blocking collectives, exchange(): lax.all_to_all(payload, axis, 0, 0, axis_index_groups=[order], tiled=True)  10.3 us
    pallas_call x6, Pallas kernels, call(): pl.pallas_call(kernel, out_shape=outs, in_specs=[smem if a.ndim == 1 else...  8.35 us
    all_to_all x2, waiting for transfers between devices, exchange(): lax.all_to_all(payload, axis, 0, 0, axis_index_groups=[order], tiled=True)  4.6 us
  transfers between devices with their start and end apart: 2, of which 1 were waited for; matrix products, arithmetic and copies ran while one was open for 0% of the time, Pallas kernels for 6%

profile of v7, /device:TPU:1, one launch (start us, length us, event | category | flops | bytes accessed | tf_op | source)
XLA Modules:
  0.0 43.5 jit_solution(12812854758670212485)
XLA Ops:
  0.6 2.8 %shard_map.76 = f32[32,8,128]{2,1,0:T(8,128)} custom-call(s32[4,2048]{1,0:T(4,128)} %boxes_ref.1, s32[1,2048]{1,0:T(1,128)} %bitcast.21), custom_call_target="tpu_custom_call" | custom-call | flops 1000000 | bytes 1000000 | tf_op jit(solution)/shard_map/pallas_call | solution.py:293
  3.4 0.0 copy-start
  3.4 0.0 copy-start.1
  3.4 11.6 %all-to-all-start.2 = ((f32[32,8,128]{2,1,0:T(8,128)}), f32[32,8,128]{2,1,0:T(8,128)S(1)}, u32[]{:S(2)}, u32[]{:S(2)}) async-start(f32[32,8,128]{2,1,0:T(8,128)} %shard_map.76), calls=%async_computation.2 | async-start | bytes 262144 | tf_op jit(solution)/shard_map/all_to_all | solution.py:336
  15.1 0.0 copy-done
  15.1 0.0 copy-done.1
  15.1 0.0 copy-start.2
  15.1 1.3 %shard_map.77 = (f32[512,128]{1,0:T(8,128)S(1)}, f32[8,128]{1,0:T(8,128)S(1)}) custom-call(s32[1,2048]{1,0:T(1,128)S(1)} %copy-done, f32[1,2048]{1,0:T(1,128)S(1)} %copy-done.1), custom_call_target="tpu_custom_call" | custom-call | flops 4000000000 | bytes 1000000 | tf_op jit(solution)/shard_map/pallas_call | solution.py:293
  16.4 4.6 %all-to-all-done.2.nets_ref = f32[32,8,128]{2,1,0:T(8,128)S(1)} async-done(((f32[32,8,128]{2,1,0:T(8,128)}), f32[32,8,128]{2,1,0:T(8,128)S(1)}, u32[]{:S(2)}, u32[]{:S(2)}) %all-to-all-start.2) | async-done | bytes 131104 | tf_op jit(solution)/shard_map/all_to_all | solution.py:336
  21.0 0.0 copy-done.2
  21.0 1.4 %shard_map.78 = (f32[512,128]{1,0:T(8,128)S(1)}, f32[128,128]{1,0:T(8,128)S(1)}) custom-call(f32[32,8,128]{2,1,0:T(8,128)S(1)} %all-to-all-done.2.nets_ref, f32[512,128]{1,0:T(8,128)S(1)} %copy-done.2, f32[512,128]{1,0:T(8,128)S(1)} %get-tuple-element.109.below_ref, f32[8,128]{1,0:T(8,128)S(1)} %get-tuple-element.110.sums_ref), custom_call_target="tpu_custom_call" | custom-call | flops 1000000 | bytes 1000000 | tf_op jit(solution)/shard_map/pallas_call | solution.py:293
  22.3 10.3 %all_to_all.30 = f32[32,4,128]{2,1,0:T(4,128)S(1)} all-to-all(f32[32,4,128]{2,1,0:T(4,128)S(1)} %bitcast.16), channel_id=1, replica_groups={{161,0,1,2,34,64,192,3,35,65,193,32,66,98,128,194,226,33,67,99,129,195,..., dimensions={0} | all-to-all | bytes 131072 | tf_op jit(solution)/shard_map/all_to_all | solution.py:336
  32.7 0.0 copy-start.4
  32.7 0.7 %shard_map.79 = (f32[8,128]{1,0:T(8,128)}, f32[8,128]{1,0:T(8,128)}, s32[1]{0:T(128)}, s32[1]{0:T(128)}) custom-call(f32[128,128]{1,0:T(8,128)S(1)} %bitcast.15), custom_call_target="tpu_custom_call" | custom-call | flops 1000000 | bytes 1000000 | tf_op jit(solution)/shard_map/pallas_call | solution.py:293
  33.4 0.0 copy-start.5
  34.0 0.0 copy-done.4
  34.1 0.0 copy-done.5
  34.1 0.0 copy-start.3
  34.1 0.0 copy-start.6
  34.1 7.1 %all-to-all-start.4 = ((f32[8,1,128]{2,1,0:T(1,128)}), f32[8,1,128]{2,1,0:T(1,128)S(1)}, u32[]{:S(2)}, u32[]{:S(2)}) async-start(f32[8,1,128]{2,1,0:T(1,128)} %bitcast.7), calls=%async_computation.4 | async-start | bytes 8192 | tf_op jit(solution)/shard_map/all_to_all | solution.py:336
  41.3 0.0 copy-done.6
  41.3 1.5 %shard_map.80 = (f32[512,128]{1,0:T(8,128)}, f32[1,2048]{1,0:T(1,128)S(1)}) custom-call(f32[512,128]{1,0:T(8,128)S(1)} %get-tuple-element.106.rudy_ref, f32[512,128]{1,0:T(8,128)S(1)} %copy-done.2, s32[1,2048]{1,0:T(1,128)S(1)} %copy-done, f32[8,128]{1,0:T(8,128)S(1)} %copy-done.6), custom_call_target="tpu_custom_call" | custom-call | flops 4000000000 | bytes 1000000 | tf_op jit(solution)/shard_map/pallas_call | solution.py:293
  42.7 0.0 copy-done.3
  42.7 0.0 all-to-all-done.4
  42.7 0.7 %shard_map.81 = f32[16,128]{1,0:T(8,128)} custom-call(f32[8,128]{1,0:T(8,128)S(1)} %copy-done.6, f32[8,128]{1,0:T(8,128)S(1)} %bitcast.17, s32[16,128]{1,0:T(8,128)S(1)} %bitcast.18, f32[16,128]{1,0:T(8,128)S(1)} %bitcast.19, f32[16,128]{1,0:T(8,128)S(1)} %bitcast.20), custom_call_target="tpu_custom_call" | custom-call | flops 1000000 | bytes 1000000 | tf_op jit(solution)/shard_map/pallas_call | solution.py:293
  (1 shorter events, 0.0 us)
Async XLA Ops:
  3.4 11.6 %copy-start = (s32[1,2048]{1,0:T(1,128)S(1)}, s32[1,2048]{1,0:T(1,128)}, u32[]{:S(2)}) copy-start(s32[1,2048]{1,0:T(1,128)} %bins_ref.3) | copy-start | bytes 24580
  3.4 11.6 %copy-start.1 = (f32[1,2048]{1,0:T(1,128)S(1)}, f32[1,2048]{1,0:T(1,128)}, u32[]{:S(2)}) copy-start(f32[1,2048]{1,0:T(1,128)} %area_ref.1) | copy-start | bytes 24580
  3.4 17.6 %all-to-all-start.2 = ((f32[32,8,128]{2,1,0:T(8,128)}), f32[32,8,128]{2,1,0:T(8,128)S(1)}, u32[]{:S(2)}, u32[]{:S(2)}) async-start(f32[32,8,128]{2,1,0:T(8,128)} %shard_map.76), calls=%async_computation.2 | async-start | bytes 262144 | tf_op jit(solution)/shard_map/all_to_all | solution.py:336
  15.1 5.9 %copy-start.2 = (f32[512,128]{1,0:T(8,128)S(1)}, f32[512,128]{1,0:T(8,128)}, u32[]{:S(2)}) copy-start(f32[512,128]{1,0:T(8,128)} %capacity_ref.3) | copy-start | bytes 786436
  32.7 1.4 %copy-start.4 = (s32[4,2048]{1,0:T(4,128)S(1)}, s32[4,2048]{1,0:T(4,128)}, u32[]{:S(2)}) copy-start(s32[4,2048]{1,0:T(4,128)} %boxes_ref.1) | copy-start | bytes 98308
  33.4 0.7 %copy-start.5 = (s32[2048]{0:T(1024)S(1)}, s32[2048]{0:T(1024)}, u32[]{:S(2)}) copy-start(s32[2048]{0:T(1024)} %param.10) | copy-start | bytes 24580
  34.1 8.6 %copy-start.3 = (f32[512,128]{1,0:T(8,128)}, f32[512,128]{1,0:T(8,128)S(1)}, u32[]{:S(2)}) copy-start(f32[512,128]{1,0:T(8,128)S(1)} %get-tuple-element.106.rudy_ref) | copy-start | bytes 786436
  34.1 7.2 %copy-start.6 = (f32[8,128]{1,0:T(8,128)S(1)}, f32[8,128]{1,0:T(8,128)}, u32[]{:S(2)}) copy-start(f32[8,128]{1,0:T(8,128)} %get-tuple-element.118.carried_ref) | copy-start | bytes 12292
  34.1 8.6 %all-to-all-start.4 = ((f32[8,1,128]{2,1,0:T(1,128)}), f32[8,1,128]{2,1,0:T(1,128)S(1)}, u32[]{:S(2)}, u32[]{:S(2)}) async-start(f32[8,1,128]{2,1,0:T(1,128)} %bitcast.7), calls=%async_computation.4 | async-start | bytes 8192 | tf_op jit(solution)/shard_map/all_to_all | solution.py:336

commit v8 on v7

--- a/solution.py
+++ b/solution.py
@@ -88,16 +88,20 @@
 
     slot = iota((SLOTS, nets), 0).astype(F32).astype(BF16)
     field = iota((8, SLOTS), 0)
-    for group in range(groups):
-        mine = jnp.broadcast_to(rank[group : group + 1, :], (16, nets)).astype(BF16)
-        mine = jnp.concatenate([mine] * (SLOTS // 16), axis=0)
-        chosen = jnp.where(slot == mine, BF16(1), BF16(0))
-        got = contract(vals, chosen, 1, 1)
-        row = got[0:8] * 256.0 + got[8:16]
-        row = jnp.where(field == 5, jnp.broadcast_to(largest, (8, SLOTS)), row)
-        for at, peer in enumerate(order):
-            if peer * groups // peers == group:
-                out_ref[at] = row
+    for pair in range(0, groups, 2):
+        chosen = []
+        for group in (pair, pair + 1):
+            mine = jnp.broadcast_to(rank[group : group + 1, :], (16, nets)).astype(BF16)
+            mine = jnp.concatenate([mine] * (SLOTS // 16), axis=0)
+            chosen.append(jnp.where(slot == mine, BF16(1), BF16(0)))
+        both = contract(vals, jnp.concatenate(chosen, axis=0), 1, 1)
+        for group in (pair, pair + 1):
+            got = both[:, (group - pair) * SLOTS : (group - pair + 1) * SLOTS]
+            row = got[0:8] * 256.0 + got[8:16]
+            row = jnp.where(field == 5, jnp.broadcast_to(largest, (8, SLOTS)), row)
+            for at, peer in enumerate(order):
+                if peer * groups // peers == group:
+                    out_ref[at] = row
 
 
 def cells_kernel(tile_rows, tile_cols, bins_ref, area_ref, below_ref, sums_ref):
@@ -166,7 +170,7 @@
         (row_start + first).astype(F32) for first in range(0, tile_rows, half)
     ]
     rudy = jnp.zeros((tile_rows, tile_cols), F32)
-    step = 4
+    step = 8
     for peer in range(0, peers, step):
         hits, cols = [], []
         for box in [nets_ref[peer + k] for k in range(step)]:

time: 43.9 us -> 43.9 us (level)
  no operation moved by 1% of the time
where the time goes in v8:
time: 43.9 us; the launch traced here: 43.4 us
  starting transfers between devices  18.8 us (43%)
  blocking collectives  10.3 us (23%)
  Pallas kernels  8.34 us (19%)
  waiting for transfers between devices  4.61 us (11%)
  between operations  1.34 us (3%)
    all_to_all x2, starting transfers between devices, exchange(): lax.all_to_all(payload, axis, 0, 0, axis_index_groups=[order], tiled=True)  18.8 us
    all_to_all x1, blocking collectives, exchange(): lax.all_to_all(payload, axis, 0, 0, axis_index_groups=[order], tiled=True)  10.3 us
    pallas_call x6, Pallas kernels, call(): pl.pallas_call(kernel, out_shape=outs, in_specs=[smem if a.ndim == 1 else...  8.34 us
    all_to_all x2, waiting for transfers between devices, exchange(): lax.all_to_all(payload, axis, 0, 0, axis_index_groups=[order], tiled=True)  4.61 us
  transfers between devices with their start and end apart: 2, of which 1 were waited for; matrix products, arithmetic and copies ran while one was open for 0% of the time, Pallas kernels for 6%

profile of v8, /device:TPU:1, one launch (start us, length us, event | category | flops | bytes accessed | tf_op | source)
XLA Modules:
  0.0 43.4 jit_solution(6169965338785305001)
XLA Ops:
  0.6 2.8 %shard_map.76 = f32[32,8,128]{2,1,0:T(8,128)} custom-call(s32[4,2048]{1,0:T(4,128)} %boxes_ref.1, s32[1,2048]{1,0:T(1,128)} %bitcast.21), custom_call_target="tpu_custom_call" | custom-call | flops 1000000 | bytes 1000000 | tf_op jit(solution)/shard_map/pallas_call | solution.py:297
  3.4 0.0 copy-start
  3.4 0.0 copy-start.1
  3.4 11.6 %all-to-all-start.2 = ((f32[32,8,128]{2,1,0:T(8,128)}), f32[32,8,128]{2,1,0:T(8,128)S(1)}, u32[]{:S(2)}, u32[]{:S(2)}) async-start(f32[32,8,128]{2,1,0:T(8,128)} %shard_map.76), calls=%async_computation.2 | async-start | bytes 262144 | tf_op jit(solution)/shard_map/all_to_all | solution.py:340
  15.0 0.0 copy-done
  15.0 0.0 copy-done.1
  15.1 0.0 copy-start.2
  15.1 1.3 %shard_map.77 = (f32[512,128]{1,0:T(8,128)S(1)}, f32[8,128]{1,0:T(8,128)S(1)}) custom-call(s32[1,2048]{1,0:T(1,128)S(1)} %copy-done, f32[1,2048]{1,0:T(1,128)S(1)} %copy-done.1), custom_call_target="tpu_custom_call" | custom-call | flops 4000000000 | bytes 1000000 | tf_op jit(solution)/shard_map/pallas_call | solution.py:297
  16.4 4.6 %all-to-all-done.2.nets_ref = f32[32,8,128]{2,1,0:T(8,128)S(1)} async-done(((f32[32,8,128]{2,1,0:T(8,128)}), f32[32,8,128]{2,1,0:T(8,128)S(1)}, u32[]{:S(2)}, u32[]{:S(2)}) %all-to-all-start.2) | async-done | bytes 131104 | tf_op jit(solution)/shard_map/all_to_all | solution.py:340
  21.0 0.0 copy-done.2
  21.0 1.4 %shard_map.78 = (f32[512,128]{1,0:T(8,128)S(1)}, f32[128,128]{1,0:T(8,128)S(1)}) custom-call(f32[32,8,128]{2,1,0:T(8,128)S(1)} %all-to-all-done.2.nets_ref, f32[512,128]{1,0:T(8,128)S(1)} %copy-done.2, f32[512,128]{1,0:T(8,128)S(1)} %get-tuple-element.109.below_ref, f32[8,128]{1,0:T(8,128)S(1)} %get-tuple-element.110.sums_ref), custom_call_target="tpu_custom_call" | custom-call | flops 1000000 | bytes 1000000 | tf_op jit(solution)/shard_map/pallas_call | solution.py:297
  22.3 10.3 %all_to_all.30 = f32[32,4,128]{2,1,0:T(4,128)S(1)} all-to-all(f32[32,4,128]{2,1,0:T(4,128)S(1)} %bitcast.16), channel_id=1, replica_groups={{161,0,1,2,34,64,192,3,35,65,193,32,66,98,128,194,226,33,67,99,129,195,..., dimensions={0} | all-to-all | bytes 131072 | tf_op jit(solution)/shard_map/all_to_all | solution.py:340
  32.7 0.0 copy-start.4
  32.7 0.7 %shard_map.79 = (f32[8,128]{1,0:T(8,128)}, f32[8,128]{1,0:T(8,128)}, s32[1]{0:T(128)}, s32[1]{0:T(128)}) custom-call(f32[128,128]{1,0:T(8,128)S(1)} %bitcast.15), custom_call_target="tpu_custom_call" | custom-call | flops 1000000 | bytes 1000000 | tf_op jit(solution)/shard_map/pallas_call | solution.py:297
  33.4 0.0 copy-start.5
  34.0 0.0 copy-done.4
  34.0 0.0 copy-done.5
  34.1 0.0 copy-start.3
  34.1 0.0 copy-start.6
  34.1 7.1 %all-to-all-start.4 = ((f32[8,1,128]{2,1,0:T(1,128)}), f32[8,1,128]{2,1,0:T(1,128)S(1)}, u32[]{:S(2)}, u32[]{:S(2)}) async-start(f32[8,1,128]{2,1,0:T(1,128)} %bitcast.7), calls=%async_computation.4 | async-start | bytes 8192 | tf_op jit(solution)/shard_map/all_to_all | solution.py:340
  41.2 0.0 copy-done.6
  41.2 1.5 %shard_map.80 = (f32[512,128]{1,0:T(8,128)}, f32[1,2048]{1,0:T(1,128)S(1)}) custom-call(f32[512,128]{1,0:T(8,128)S(1)} %get-tuple-element.106.rudy_ref, f32[512,128]{1,0:T(8,128)S(1)} %copy-done.2, s32[1,2048]{1,0:T(1,128)S(1)} %copy-done, f32[8,128]{1,0:T(8,128)S(1)} %copy-done.6), custom_call_target="tpu_custom_call" | custom-call | flops 4000000000 | bytes 1000000 | tf_op jit(solution)/shard_map/pallas_call | solution.py:297
  42.7 0.0 copy-done.3
  42.7 0.0 all-to-all-done.4
  42.7 0.7 %shard_map.81 = f32[16,128]{1,0:T(8,128)} custom-call(f32[8,128]{1,0:T(8,128)S(1)} %copy-done.6, f32[8,128]{1,0:T(8,128)S(1)} %bitcast.17, s32[16,128]{1,0:T(8,128)S(1)} %bitcast.18, f32[16,128]{1,0:T(8,128)S(1)} %bitcast.19, f32[16,128]{1,0:T(8,128)S(1)} %bitcast.20), custom_call_target="tpu_custom_call" | custom-call | flops 1000000 | bytes 1000000 | tf_op jit(solution)/shard_map/pallas_call | solution.py:297
  (1 shorter events, 0.0 us)
Async XLA Ops:
  3.4 11.6 %copy-start = (s32[1,2048]{1,0:T(1,128)S(1)}, s32[1,2048]{1,0:T(1,128)}, u32[]{:S(2)}) copy-start(s32[1,2048]{1,0:T(1,128)} %bins_ref.3) | copy-start | bytes 24580
  3.4 11.6 %copy-start.1 = (f32[1,2048]{1,0:T(1,128)S(1)}, f32[1,2048]{1,0:T(1,128)}, u32[]{:S(2)}) copy-start(f32[1,2048]{1,0:T(1,128)} %area_ref.1) | copy-start | bytes 24580
  3.4 17.6 %all-to-all-start.2 = ((f32[32,8,128]{2,1,0:T(8,128)}), f32[32,8,128]{2,1,0:T(8,128)S(1)}, u32[]{:S(2)}, u32[]{:S(2)}) async-start(f32[32,8,128]{2,1,0:T(8,128)} %shard_map.76), calls=%async_computation.2 | async-start | bytes 262144 | tf_op jit(solution)/shard_map/all_to_all | solution.py:340
  15.1 5.9 %copy-start.2 = (f32[512,128]{1,0:T(8,128)S(1)}, f32[512,128]{1,0:T(8,128)}, u32[]{:S(2)}) copy-start(f32[512,128]{1,0:T(8,128)} %capacity_ref.3) | copy-start | bytes 786436
  32.7 1.4 %copy-start.4 = (s32[4,2048]{1,0:T(4,128)S(1)}, s32[4,2048]{1,0:T(4,128)}, u32[]{:S(2)}) copy-start(s32[4,2048]{1,0:T(4,128)} %boxes_ref.1) | copy-start | bytes 98308
  33.4 0.7 %copy-start.5 = (s32[2048]{0:T(1024)S(1)}, s32[2048]{0:T(1024)}, u32[]{:S(2)}) copy-start(s32[2048]{0:T(1024)} %param.10) | copy-start | bytes 24580
  34.1 8.6 %copy-start.3 = (f32[512,128]{1,0:T(8,128)}, f32[512,128]{1,0:T(8,128)S(1)}, u32[]{:S(2)}) copy-start(f32[512,128]{1,0:T(8,128)S(1)} %get-tuple-element.106.rudy_ref) | copy-start | bytes 786436
  34.1 7.2 %copy-start.6 = (f32[8,128]{1,0:T(8,128)S(1)}, f32[8,128]{1,0:T(8,128)}, u32[]{:S(2)}) copy-start(f32[8,128]{1,0:T(8,128)} %get-tuple-element.118.carried_ref) | copy-start | bytes 12292
  34.1 8.6 %all-to-all-start.4 = ((f32[8,1,128]{2,1,0:T(1,128)}), f32[8,1,128]{2,1,0:T(1,128)S(1)}, u32[]{:S(2)}, u32[]{:S(2)}) async-start(f32[8,1,128]{2,1,0:T(1,128)} %bitcast.7), calls=%async_computation.4 | async-start | bytes 8192 | tf_op jit(solution)/shard_map/all_to_all | solution.py:340
